TPU v7x, 32 devices: a whole 2x2x4 slice. The times are simulated.
32 devices in a mesh: batch: 4 (over z), tensor: 8 (over y, x, core).
Axes of the slice: x: 2, y: 2, z: 4, core: 2. Of those that a mesh axis runs over, the one named last changes fastest.
Arguments:
- attn_values: bfloat16 [1024, 8192], P('batch', 'tensor'), may hold values from -6 to 6
- out_weight: bfloat16 [8192, 8192], P('tensor'), may hold values from -0.09375 to 0.09375
- residual_t: bfloat16 [8192, 1024], P('tensor', 'batch'), may hold values from -6 to 6
- projector: bfloat16 [8192, 4096], P('tensor'), may hold values from -0.0625 to 0.0625
- student_input: bfloat16 [1024, 4096], P('batch', 'tensor'), may hold values from -6 to 6
- norm_gain: float32 [4096], replicated, may hold values from 0.1 to 1.9
- w_gate: bfloat16 [4096, 8192], P('batch', 'tensor'), may hold values from -0.09375 to 0.09375
- w_up: bfloat16 [4096, 8192], P('batch', 'tensor'), may hold values from -0.09375 to 0.09375
- w_down: bfloat16 [4096, 8192], P('batch', 'tensor'), may hold values from -0.0625 to 0.0625
- route_index: int32 [4, 64], P('batch'), may hold values from -1 to 255, as said below
Outputs:
- teacher_hidden: bfloat16 [8192, 1024], P('tensor', 'batch')
- grad_gate: float32 [4096, 8192], P('batch', 'tensor')
- grad_up: float32 [4096, 8192], P('batch', 'tensor')
- grad_down: float32 [4096, 8192], P('batch', 'tensor')
Inputs may be any that keep to these rules, and one draw needn't show every extreme that they name: `route_index`: in each batch group the live slots come first, hold distinct positions in increasing order, and the empty slots after them hold -1. The batch groups hold 128 live slots together, and some batch group has all 64 slots live.
All inputs are finite; a program needn't handle non-finite values.
Results may differ from a plain program's by a relative error of at most 0.025.
Values may be sent and summed in bfloat16 or wider, within the bound.
A program may use at most 128 MiB of HBM per device.

v0:
```python
import functools
import math

import jax
import jax.numpy as jnp
from jax import lax
from jax.experimental import pallas as pl
from jax.experimental.pallas import tpu as pltpu
from jax.sharding import PartitionSpec as P

epsilon = 1e-05
f32 = jnp.float32
bf16 = jnp.bfloat16


def contract(left, right, left_dim, right_dim):
    return lax.dot_general(
        left, right, (((left_dim,), (right_dim,)), ((), ())), preferred_element_type=f32
    )


VMEM = pl.BlockSpec(memory_space=pltpu.VMEM)


def meet(axis, size):
    me = lax.axis_index(axis)
    barrier = pltpu.get_barrier_semaphore()
    for step in range(1, size):
        pl.semaphore_signal(
            barrier,
            inc=1,
            device_id={axis: lax.rem(me + step, size)},
            device_id_type=pl.DeviceIdType.MESH,
        )
    pl.semaphore_wait(barrier, size - 1)
    return me


def send(source, land, send_sem, recv_sem, axis, size, me):
    copies = []
    for step in range(1, size):
        peer = lax.rem(me + step, size)
        copy = pltpu.make_async_remote_copy(
            src_ref=source(peer),
            dst_ref=land.at[step - 1],
            send_sem=send_sem.at[step - 1],
            recv_sem=recv_sem.at[step - 1],
            device_id={axis: peer},
            device_id_type=pl.DeviceIdType.MESH,
        )
        copy.start()
        copies.append(copy)
    return copies


def exchange_kernel(axis, size, gather, x, out, land, send_sem, recv_sem):
    me = meet(axis, size)
    source = (lambda peer: x) if gather else (lambda peer: x.at[peer])
    copies = send(source, land, send_sem, recv_sem, axis, size, me)
    out[me] = x[...] if gather else x[me]
    for step in range(1, size):
        copies[step - 1].wait()
        out[lax.rem(me + size - step, size)] = land[step - 1]


def sum_kernel(axis, size, scale, x, out, land, share, late, sems):
    me = meet(axis, size)
    first = send(lambda peer: x.at[peer], land, sems.at[0], sems.at[1], axis, size, me)
    total = x[me].astype(f32)
    for step in range(1, size):
        first[step - 1].wait()
        total = total + land[step - 1].astype(f32)
    share[...] = (total * scale).astype(bf16)
    second = send(lambda peer: share, late, sems.at[2], sems.at[3], axis, size, me)
    out[me] = share[...]
    for step in range(1, size):
        second[step - 1].wait()
        out[lax.rem(me + size - step, size)] = late[step - 1]


def exchange(x, axis, ident, gather=False):
    size = lax.axis_size(axis)
    block = x.shape if gather else x.shape[1:]
    return pl.pallas_call(
        functools.partial(exchange_kernel, axis, size, gather),
        out_shape=jax.ShapeDtypeStruct((size,) + block, x.dtype),
        in_specs=[VMEM],
        out_specs=VMEM,
        scratch_shapes=[
            pltpu.VMEM((size - 1,) + block, x.dtype),
            pltpu.SemaphoreType.DMA((size - 1,)),
            pltpu.SemaphoreType.DMA((size - 1,)),
        ],
        compiler_params=pltpu.CompilerParams(collective_id=ident, has_side_effects=True),
    )(x)


def all_sum(terms, axis, ident, scale=1.0):
    size = lax.axis_size(axis)
    shares = terms.reshape((size, terms.shape[0] // size) + terms.shape[1:])
    block = shares.shape[1:]
    return pl.pallas_call(
        functools.partial(sum_kernel, axis, size, scale),
        out_shape=jax.ShapeDtypeStruct(shares.shape, bf16),
        in_specs=[VMEM],
        out_specs=VMEM,
        scratch_shapes=[
            pltpu.VMEM((size - 1,) + block, bf16),
            pltpu.VMEM(block, bf16),
            pltpu.VMEM((size - 1,) + block, bf16),
            pltpu.SemaphoreType.DMA((4, size - 1)),
        ],
        compiler_params=pltpu.CompilerParams(collective_id=ident, has_side_effects=True),
    )(shares).reshape(terms.shape)


def on_device(
    attn_values,
    out_weight,
    residual_t,
    projector,
    student_input,
    norm_gain,
    w_gate,
    w_up,
    w_down,
    route_index,
):
    group_count = lax.axis_size("batch")
    mean_routed = student_input.shape[0] // 8
    routed = mean_routed * group_count
    loss_scale = 1.0 / math.sqrt(routed)

    every_route = exchange(
        jnp.pad(route_index, ((0, 7), (0, -route_index.shape[1] % 128)), constant_values=-1),
        "batch",
        1,
        gather=True,
    )[:, 0, : route_index.shape[1]].reshape(-1)
    live = every_route >= 0
    rank = jnp.cumsum(live.astype(jnp.int32)) - 1
    row_ids = lax.broadcasted_iota(jnp.int32, (routed, live.shape[0]), 0)
    select = ((rank[None, :] == row_ids) & live[None, :]).astype(bf16)
    live_row = lax.broadcasted_iota(jnp.int32, (routed, 1), 0) <= rank[-1]

    slot_pos = route_index[0]
    present = slot_pos >= 0
    safe_slot = jnp.maximum(slot_pos, 0)
    local_rows = jnp.where(present[:, None], jnp.take(student_input, safe_slot, axis=0), 0)
    routed_input = exchange(local_rows, "tensor", 2, gather=True).astype(f32)
    width = routed_input.shape[0] * routed_input.shape[2]
    mean_square = jnp.sum(routed_input * routed_input, axis=(0, 2), keepdims=True) / width
    gain = norm_gain.reshape(routed_input.shape[0], 1, -1)
    normed = (routed_input * lax.rsqrt(mean_square + epsilon) * gain).astype(bf16)
    normed = jnp.swapaxes(normed, 0, 1).reshape(slot_pos.shape[0], group_count, -1)
    every_normed = exchange(jnp.swapaxes(normed, 0, 1), "batch", 3)
    every_normed = every_normed.reshape(live.shape[0], -1)

    summed = lax.psum_scatter(
        contract(out_weight, attn_values, 0, 1).astype(bf16),
        "tensor",
        scatter_dimension=0,
        tiled=True,
    ).astype(f32)
    teacher_hidden = (residual_t.astype(f32) + summed).astype(bf16)

    rows = contract(select, every_normed, 1, 0).astype(bf16)
    gate_up = jnp.concatenate([contract(rows, w_gate, 1, 0), contract(rows, w_up, 1, 0)])
    gate_up = all_sum(gate_up.astype(bf16), "batch", 4).astype(f32)
    gate_act, up_act = gate_up[:routed], gate_up[routed:]
    sigma_gate = jax.nn.sigmoid(gate_act)
    hidden = (gate_act * sigma_gate * up_act).astype(bf16)
    out_part = contract(hidden, w_down, 1, 1)

    routed_teacher = jnp.where(present[None, :], jnp.take(teacher_hidden, safe_slot, axis=1), 0)
    target_part = contract(routed_teacher, projector, 0, 0).astype(bf16)
    target_part = target_part.reshape(slot_pos.shape[0], group_count, -1)
    every_target = exchange(jnp.swapaxes(target_part, 0, 1), "batch", 5)
    every_target = every_target.reshape(live.shape[0], -1)
    target_rows = contract(select, every_target, 1, 0)

    misfit = jnp.where(live_row, out_part - target_rows, 0.0)
    grad_out = all_sum(misfit.astype(bf16), "tensor", 6, loss_scale)
    grad_hidden = all_sum(contract(grad_out, w_down, 1, 0).astype(bf16), "batch", 7).astype(f32)
    grad_gate_act = (
        grad_hidden * up_act * sigma_gate * (1.0 + gate_act * (1.0 - sigma_gate))
    ).astype(bf16)
    grad_up_act = (grad_hidden * gate_act * sigma_gate).astype(bf16)
    grad_gate = contract(rows, grad_gate_act, 0, 0)
    grad_up = contract(rows, grad_up_act, 0, 0)
    grad_down = contract(grad_out, hidden, 0, 0)
    return (teacher_hidden, grad_gate, grad_up, grad_down)


def solution(mesh):
    in_specs = (
        P("batch", "tensor"),
        P("tensor", None),
        P("tensor", "batch"),
        P("tensor", None),
        P("batch", "tensor"),
        P(),
        P("batch", "tensor"),
        P("batch", "tensor"),
        P("batch", "tensor"),
        P("batch", None),
    )
    out_specs = (
        P("tensor", "batch"),
        P("batch", "tensor"),
        P("batch", "tensor"),
        P("batch", "tensor"),
    )
    return jax.shard_map(
        on_device, mesh=mesh, in_specs=in_specs, out_specs=out_specs, check_vma=False
    )
```

profile of v0, /device:TPU:0, one launch (start us, length us, event | category | flops | bytes accessed | tf_op | source)
XLA Modules:
  0.0 184.7 jit_solution(17022893312981474006)
XLA Ops:
  7.2 0.0 reduce-scatter.2.cloned.1.call-start
  7.2 12.8 %convolution_convert_fusion = bf16[8192,256]{1,0:T(8,128)(2,1)} fusion(bf16[1024,8192]{1,0:T(8,128)(2,1)} %param.11, bf16[256,1024]{1,0:T(8,128)(2,1)} %param.10), kind=kOutput, calls=%fused_computation.2 | convolution fusion | flops 4297064448 | bytes 21495808 | tf_op jit(solution)/shard_map/dot_general | solution.py:17
  20.0 0.6 copy-done.10
  20.7 0.6 pad.4.x
  21.3 8.6 %shard_map.129 = s32[4,8,128]{2,1,0:T(8,128)} custom-call(s32[8,128]{1,0:T(8,128)} %pad.4.x), custom_call_target="tpu_custom_call" | custom-call | tf_op jit(solution)/shard_map/pallas_call | solution.py:84
  29.9 0.7 fusion.29
  30.6 0.1 reshape.128
  30.7 0.7 compare_reduce_fusion
  31.4 0.1 ge.39
  31.5 0.3 reduce-window.9
  31.8 0.1 slice.26
  31.9 0.1 slice_reduce_fusion
  32.1 0.1 add_bitcast_fusion
  32.1 0.6 slice.28
  32.8 0.7 gather_fusion
  33.5 0.7 select_select_fusion.x
  34.2 10.6 %shard_map.130 = bf16[8,64,512]{2,1,0:T(8,128)(2,1)} custom-call(bf16[64,512]{1,0:T(8,128)(2,1)} %select_select_fusion.x), custom_call_target="tpu_custom_call" | custom-call | tf_op jit(solution)/shard_map/pallas_call | solution.py:84
  44.8 1.4 fusion.2
  46.2 1.2 fusion.10
  47.5 0.3 copy.15
  47.8 0.3 reshape.121
  48.1 1.0 copy.23
  49.1 15.5 %shard_map.131 = bf16[4,64,1024]{2,1,0:T(8,128)(2,1)} custom-call(bf16[4,64,1024]{2,1,0:T(8,128)(2,1)} %bitcast.83), custom_call_target="tpu_custom_call" | custom-call | tf_op jit(solution)/shard_map/pallas_call | solution.py:84
  64.5 1.4 convolution_convert_fusion.5
  66.0 2.0 %convolution_convert_fusion.3 = bf16[128,1024]{1,0:T(8,128)(2,1)S(1)} fusion(bf16[128,1024]{1,0:T(8,128)(2,1)S(1)} %convolution_convert_fusion.5, bf16[1024,1024]{1,0:T(8,128)(2,1)} %param.17), kind=kOutput, calls=%fused_computation.10 | convolution fusion | flops 268566528 | bytes 2621440 | tf_op jit(solution)/shard_map/dot_general | solution.py:17
  68.0 2.0 %convolution_convert_fusion.4 = bf16[128,1024]{1,0:T(8,128)(2,1)S(1)} fusion(bf16[128,1024]{1,0:T(8,128)(2,1)S(1)} %convolution_convert_fusion.5, bf16[1024,1024]{1,0:T(8,128)(2,1)} %param.16), kind=kOutput, calls=%fused_computation.11 | convolution fusion | flops 268566528 | bytes 2621440 | tf_op jit(solution)/shard_map/dot_general | solution.py:17
  70.1 0.8 pad_maximum_fusion
  70.9 29.0 %shard_map.132 = bf16[4,64,1024]{2,1,0:T(8,128)(2,1)} custom-call(bf16[4,64,1024]{2,1,0:T(8,128)(2,1)} %bitcast.82), custom_call_target="tpu_custom_call" | custom-call | tf_op jit(solution)/shard_map/pallas_call | solution.py:102
  99.9 1.2 iota_compare_fusion.1
  101.1 1.1 fusion.32
  102.2 0.8 copy-done.1
  103.0 0.2 fusion.11
  103.2 0.7 copy-done.3
  103.9 1.6 fusion.33
  105.5 2.0 %add_convert_fusion = bf16[1024,256]{1,0:T(8,128)(2,1)} fusion(bf16[1024,256]{1,0:T(8,128)(2,1)} %reduce-scatter.2.cloned.1.call-done, bf16[1024,256]{1,0:T(8,128)(2,1)S(1)} %copy-done.6), kind=kLoop, calls=%fused_computation.16 | loop fusion | flops 1048576 | bytes 1572864 | tf_op jit(solution)/shard_map/convert_element_type | solution.py:165
  107.5 1.2 copy.17
  108.7 0.7 gather_fusion.1
  109.5 5.1 %convolution_convert_fusion.1 = bf16[64,4096]{1,0:T(8,128)(2,1)S(1)} fusion(bf16[1024,4096]{1,0:T(8,128)(2,1)} %param.13, bf16[64,1024]{1,0:T(8,128)(2,1)S(1)} %gather_fusion.1, pred[64]{0:T(512)(128)(4,1)S(1)} %get-tuple-element.8, pred[64]{0:T(512)(128)(4,1)S(1)} %get-tuple-element.9), kind=kOutput, calls=%fused_computation.3 | convolution fusion | flops 537264128 | bytes 9044096 | tf_op jit(solution)/shard_map/dot_general | solution.py:17
  114.5 0.8 copy.22
  115.4 15.5 %shard_map.133 = bf16[4,64,1024]{2,1,0:T(8,128)(2,1)} custom-call(bf16[4,64,1024]{2,1,0:T(8,128)(2,1)} %bitcast.85), custom_call_target="tpu_custom_call" | custom-call | tf_op jit(solution)/shard_map/pallas_call | solution.py:84
  130.9 2.0 %fusion.1 = bf16[128,1024]{1,0:T(8,128)(2,1)} fusion(f32[128,1024]{1,0:T(8,128)S(1)} %copy-done.4, bf16[256,1024]{1,0:T(8,128)(2,1)} %bitcast.80, pred[128]{0:T(512)(128)(4,1)} %iota_compare_fusion.1, s32[256]{0:T(256)S(1)} %add_bitcast_fusion, pred[256]{0:T(512)(128)(4,1)S(1)} %copy-done.9), kind=kOutput, calls=%fused_computation.8 | convolution fusion | flops 67567616 | bytes 1312128 | tf_op jit(solution)/shard_map/dot_general | solution.py:17
  132.9 13.5 %shard_map.134 = bf16[8,16,1024]{2,1,0:T(8,128)(2,1)} custom-call(bf16[8,16,1024]{2,1,0:T(8,128)(2,1)} %bitcast.86), custom_call_target="tpu_custom_call" | custom-call | tf_op jit(solution)/shard_map/pallas_call | solution.py:102
  146.4 2.1 %convolution_convert_fusion.2 = bf16[128,1024]{1,0:T(8,128)(2,1)} fusion(bf16[128,1024]{1,0:T(8,128)(2,1)} %bitcast.78, bf16[1024,1024]{1,0:T(8,128)(2,1)S(1)} %copy-done), kind=kOutput, calls=%fused_computation.9 | convolution fusion | flops 268566528 | bytes 2621440 | tf_op jit(solution)/shard_map/dot_general | solution.py:17
  148.5 3.8 %fusion.36 = f32[1024,1024]{1,0:T(8,128)} fusion(bf16[128,1024]{1,0:T(8,128)(2,1)} %bitcast.79, bf16[128,1024]{1,0:T(8,128)(2,1)} %copy-done.3), kind=kOutput, calls=%fused_computation.67 | convolution fusion | flops 268435456 | bytes 4718592 | tf_op jit(solution)/shard_map/dot_general | solution.py:17
  152.3 18.9 %shard_map.135 = bf16[4,32,1024]{2,1,0:T(8,128)(2,1)} custom-call(bf16[4,32,1024]{2,1,0:T(8,128)(2,1)} %bitcast.87), custom_call_target="tpu_custom_call" | custom-call | tf_op jit(solution)/shard_map/pallas_call | solution.py:102
  171.2 1.2 fusion.9
  172.4 2.7 %fusion.35 = f32[1024,1024]{1,0:T(8,128)} fusion(bf16[128,1024]{1,0:T(8,128)(2,1)S(1)} %convolution_convert_fusion.5, bf16[128,1024]{1,0:T(8,128)(2,1)S(1)} %get-tuple-element.4), kind=kOutput, calls=%fused_computation.66 | convolution fusion | flops 268435456 | bytes 4718592 | tf_op jit(solution)/shard_map/dot_general | solution.py:17
  175.1 2.7 %fusion.34 = f32[1024,1024]{1,0:T(8,128)} fusion(bf16[128,1024]{1,0:T(8,128)(2,1)S(1)} %convolution_convert_fusion.5, bf16[128,1024]{1,0:T(8,128)(2,1)S(1)} %get-tuple-element.5), kind=kOutput, calls=%fused_computation.65 | convolution fusion | flops 268435456 | bytes 4718592 | tf_op jit(solution)/shard_map/dot_general | solution.py:17
  (27 shorter events, 0.1 us)
Async XLA Ops:
  7.2 96.7 %copy-start = (bf16[1024,1024]{1,0:T(8,128)(2,1)S(1)}, bf16[1024,1024]{1,0:T(8,128)(2,1)}, u32[]{:S(2)}) copy-start(bf16[1024,1024]{1,0:T(8,128)(2,1)} %param.18) | copy-start | bytes 6291460
  7.2 98.3 %reduce-scatter.2.cloned.1.call-start = ((), (), s32[]{:S(2)}) async-start(), calls=%async_computation.1 | async-start | bytes 4718592 | tf_op jit(solution)/shard_map/reduce_scatter | solution.py:159
  20.0 0.7 copy-start.10
  20.0 12.7 %copy-start.7 = (f32[4096]{0:T(1024)S(1)}, f32[4096]{0:T(1024)}, u32[]{:S(2)}) copy-start(f32[4096]{0:T(1024)} %param.15) | copy-start | bytes 49156
  20.0 12.7 %copy-start.5 = (bf16[256,512]{1,0:T(8,128)(2,1)S(1)}, bf16[256,512]{1,0:T(8,128)(2,1)}, u32[]{:S(2)}) copy-start(bf16[256,512]{1,0:T(8,128)(2,1)} %param.14) | copy-start | bytes 786436
  31.5 36.5 %copy-start.8 = (pred[256]{0:T(512)(128)(4,1)}, pred[256]{0:T(512)(128)(4,1)S(1)}, u32[]{:S(2)}) copy-start(pred[256]{0:T(512)(128)(4,1)S(1)} %ge.39) | copy-start | bytes 772
  70.1 35.4 %copy-start.6 = (bf16[1024,256]{1,0:T(8,128)(2,1)S(1)}, bf16[1024,256]{1,0:T(8,128)(2,1)}, u32[]{:S(2)}) copy-start(bf16[1024,256]{1,0:T(8,128)(2,1)} %param.12) | copy-start | bytes 1572868
  102.2 0.8 copy-start.1
  103.2 0.7 copy-start.3
  109.4 21.4 %copy-start.4 = (f32[128,1024]{1,0:T(8,128)S(1)}, f32[128,1024]{1,0:T(8,128)}, u32[]{:S(2)}) copy-start(f32[128,1024]{1,0:T(8,128)} %fusion.33) | copy-start | bytes 1572868
  109.4 21.4 %copy-start.9 = (pred[256]{0:T(512)(128)(4,1)S(1)}, pred[256]{0:T(512)(128)(4,1)}, u32[]{:S(2)}) copy-start(pred[256]{0:T(512)(128)(4,1)} %copy-done.8) | copy-start | bytes 772
  132.9 38.3 %copy-start.2 = (f32[2,64,1024]{2,1,0:T(8,128)S(1)}, f32[2,64,1024]{2,1,0:T(8,128)}, u32[]{:S(2)}) copy-start(f32[2,64,1024]{2,1,0:T(8,128)} %copy-done.1) | copy-start | bytes 1572868
Sparse Core Ops, SparseCore 0:
  20.2 53.8 reduce-scatter.1
where the time goes:
time: 186 us; the launch traced here: 185 us
  Pallas kernels  112 us (60%)
  matrix products  38.3 us (21%)
  between operations  14.3 us (8%)
  other arithmetic  10.6 us (6%)
  local copies, waits for them, and re-layouts  9.86 us (5%)
    pallas_call x3, Pallas kernels, all_sum(): pl.pallas_call(functools.partial(sum_kernel, axis, size, scale), out_shap...  61.4 us
    pallas_call x4, Pallas kernels, exchange(): pl.pallas_call(functools.partial(exchange_kernel, axis, size, gather), ou...  50.1 us
    dot_general x11, matrix products, contract(): lax.dot_general(left, right, (((left_dim,), (right_dim,)), ((), ())), pre...  38.3 us
  transfers between devices with their start and end apart: 1, of which 0 were waited for; matrix products, arithmetic and copies ran while one was open for 11% of the time, Pallas kernels for 34%

commit v1 on v0

v1 whole, which is shorter than its diff:
```python
import functools
import math
import types

import jax
import jax.numpy as jnp
from jax import lax
from jax.experimental import pallas as pl
from jax.experimental.pallas import tpu as pltpu
from jax.sharding import PartitionSpec as P

epsilon = 1e-05
f32 = jnp.float32
bf16 = jnp.bfloat16
VMEM = pl.BlockSpec(memory_space=pltpu.VMEM)
ANY = pl.BlockSpec(memory_space=pl.ANY)
VMEM_BYTES = 66_000_000

NAMES = (
    "attn", "out_weight", "residual", "projector", "student", "gain", "w_gate", "w_up",
    "w_down", "route", "o_rows", "o_gate", "o_up", "o_grad", "o_hidden", "o_teacher",
    "attn_v", "weight_v", "resid_v", "proj_v", "stud_v", "wg", "wu", "wd", "load_sem",
    "q_send", "q_land", "q_sem", "t_send", "t_land", "r_acc", "r_land", "f_acc", "f_land", "t_sem", "r_sem", "f_sem",
    "c_send", "c_land", "p_acc", "p_land", "p_keep", "p_send", "p_zland", "c_sem", "p_sem", "z2_sem",
    "x_land", "sq_send", "sq_land", "count_land", "x_sem", "sq_sem", "count_sem", "z_send",
    "z_land", "z_sem", "select", "rows_v", "row_sem", "gu", "gu_land", "gu_share", "gu_sem", "gh",
    "gh_land", "gh_share", "gh_sem", "part", "m_send", "m_land", "v_share", "v_land", "m_sem",
    "v_sem", "grad_v", "g_sem",
)
PROFILE = False
open_scope = []


def mark(name):
    if not PROFILE:
        return
    while open_scope:
        open_scope.pop().__exit__(None, None, None)
    if name:
        scope = jax.named_scope(name)
        scope.__enter__()
        open_scope.append(scope)


def contract(left, right, left_dim, right_dim):
    return lax.dot_general(
        left, right, (((left_dim,), (right_dim,)), ((), ())), preferred_element_type=f32
    )


def remote(src, dst, send_sem, recv_sem, **where):
    return pltpu.make_async_remote_copy(
        src_ref=src,
        dst_ref=dst,
        send_sem=send_sem,
        recv_sem=recv_sem,
        device_id=where,
        device_id_type=pl.DeviceIdType.MESH,
    )


def start_if(cond, copy):
    @pl.when(cond)
    def _():
        copy.start()


def wait_send_if(cond, copy):
    @pl.when(cond)
    def _():
        copy.wait_send()


def wait_recv_if(cond, copy):
    @pl.when(cond)
    def _():
        copy.wait_recv()


def xor(left, right, bits):
    total = 0
    for bit in range(bits):
        step = 1 << bit
        total = total + step * lax.rem(left // step + right // step, 2)
    return total


class Chain:
    def __init__(self, own, land, share, send_sem, recv_sem, me, size):
        self.own, self.land, self.share = own, land, share
        self.send_sem, self.recv_sem = send_sem, recv_sem
        self.me, self.size, self.chunks = me, size, own.shape[0]
        self.early = jnp.where(2 * me < size, 0, 1)

    def flow(self, late):
        way = 1 - self.early if late else self.early
        before = jnp.where(way == 0, self.me, self.size - 1 - self.me) > 0
        after = jnp.where(way == 0, self.size - 1 - self.me, self.me) > 0
        peer = jnp.where(way == 0, self.me + 1, self.me - 1)
        return way, before, after, peer

    def copy(self, way, chunk, peer):
        return remote(
            self.share.at[way, chunk],
            self.land.at[way, chunk],
            self.send_sem.at[way, chunk],
            self.recv_sem.at[way, chunk],
            batch=peer,
        )

    def origin(self, first, last):
        way, before, after, peer = self.flow(False)

        @pl.when(jnp.logical_not(before))
        def _():
            for chunk in range(first, last):
                self.share[way, chunk] = self.own[chunk].astype(bf16)
                self.copy(way, chunk, peer).start()

    def step(self, chunk, late):
        way, before, after, peer = self.flow(late)
        copy = self.copy(way, chunk, peer)
        wait_recv_if(before, copy)

        @pl.when(jnp.logical_and(after, before))
        def _():
            self.share[way, chunk] = (
                self.own[chunk] + self.land[way, chunk].astype(f32)
            ).astype(bf16)
            copy.start()

    def total(self, chunk):
        @pl.when(self.me > 0)
        def _():
            self.own[chunk] = self.own[chunk] + self.land[0, chunk].astype(f32)

        @pl.when(self.me < self.size - 1)
        def _():
            self.own[chunk] = self.own[chunk] + self.land[1, chunk].astype(f32)

    def drain(self):
        for late in (False, True):
            way, _, after, peer = self.flow(late)
            for chunk in range(self.chunks):
                wait_send_if(after, self.copy(way, chunk, peer))


class PlaneScatter:
    def __init__(self, acc, land, send_sem, recv_sem, chip, core, bits):
        self.acc, self.land = acc, land
        self.send_sem, self.recv_sem = send_sem, recv_sem
        self.chip, self.core, self.bits = chip, core, bits
        self.slots, self.stages = [], []
        for half in range(2):
            order = [1 << bit for bit in range(bits)]
            order = order if half == 0 else order[::-1]
            used, slots, stages = 0, {}, []
            done = 0
            for stage, flip in enumerate(order):
                moved = [
                    block
                    for block in range((1 << bits) - 1, -1, -1)
                    if block & flip and not block & done
                ]
                for block in moved:
                    slots[(stage, block ^ flip)] = used
                    used += 1
                stages.append((flip, moved))
                done |= flip
            self.slots.append(slots)
            self.stages.append(stages)

    def copy(self, half, stage, block):
        flip, _ = self.stages[half][stage]
        slot = self.slots[half][(stage, block ^ flip)]
        return remote(
            self.acc.at[block, half],
            self.land.at[slot, half],
            self.send_sem.at[slot, half],
            self.recv_sem.at[slot, half],
            tensor=2 * xor(self.chip, flip, self.bits) + self.core,
        )

    def arrived(self, half, stages, block):
        return [
            self.land[self.slots[half][(stage, block)], half].astype(f32)
            for stage in range(stages)
        ]

    def send(self, stage):
        for half in range(2):
            for block in self.stages[half][stage][1]:
                if stage:
                    value = self.acc[block, half].astype(f32)
                    for term in self.arrived(half, stage, block):
                        value = value + term
                    self.acc[block, half] = value.astype(bf16)
                self.copy(half, stage, block).start()

    def receive(self, stage):
        for half in range(2):
            for block in self.stages[half][stage][1]:
                self.copy(half, stage, block).wait_recv()

    def final(self, half):
        value = self.acc[0, half].astype(f32)
        for term in self.arrived(half, self.bits, 0):
            value = value + term
        return value

    def drain(self):
        for half in range(2):
            for stage in range(self.bits):
                for block in self.stages[half][stage][1]:
                    self.copy(half, stage, block).wait_send()


def exchange_kernel(dims, *refs):
    (groups, tensors, mean_routed) = dims
    r = types.SimpleNamespace(**dict(zip(NAMES, refs, strict=True)))

    b, t = lax.axis_index("batch"), lax.axis_index("tensor")
    chips = tensors // 2
    bits = chips.bit_length() - 1
    chip, core = t // 2, lax.rem(t, 2)
    partner = t + 1 - 2 * core
    slots = r.route.shape[1]
    tokens, heads = r.attn.shape
    feats = r.out_weight.shape[1] // tensors
    width = r.student.shape[1]
    block = r.w_gate.shape[0]
    hidden_units = r.w_gate.shape[1]
    routed = mean_routed * groups
    tall = routed // 2
    short = routed // 4
    chunks = r.gu.shape[0] // 2
    cols = hidden_units // chunks
    others = range(1, chips)

    mark("a_loads")
    loads = {}

    def load(name, src, dst):
        copy = pltpu.make_async_copy(src, dst, r.load_sem.at[len(loads)])
        copy.start()
        loads[name] = copy

    def weight_block(index):
        place = pl.multiple_of(index * feats, feats)
        return r.out_weight.at[:, pl.ds(place, feats)]

    def owner(relative, side):
        return 2 * xor(chip, relative, bits) + (core if side else 1 - core)

    load("student", r.student, r.stud_v)
    load("attn", r.attn, r.attn_v.at[pl.ds(slots, tokens)])
    for side in range(2):
        for step in range(chips):
            place = side * chips + step
            index = owner(chips - 1 - step, side)
            load(("w", place), weight_block(index), r.weight_v.at[place])
    load("w_gate", r.w_gate, r.wg)
    load("w_up", r.w_up, r.wu)
    load("residual", r.residual, r.resid_v)
    for side in range(2):
        for step in range(chips):
            place = pl.multiple_of(owner(chips - 1 - step, side) * width, width)
            load(
                ("p", side * chips + step),
                r.projector.at[:, pl.ds(place, width)],
                r.proj_v.at[side * chips + step],
            )
    load("w_down", r.w_down, r.wd)

    barrier = pltpu.get_barrier_semaphore()
    for step in others:
        pl.semaphore_signal(
            barrier,
            inc=1,
            device_id={"tensor": 2 * xor(chip, step, bits) + core},
            device_id_type=pl.DeviceIdType.MESH,
        )
    pl.semaphore_signal(
        barrier, inc=1, device_id={"tensor": partner}, device_id_type=pl.DeviceIdType.MESH
    )
    for step in range(1, groups):
        pl.semaphore_signal(
            barrier,
            inc=1,
            device_id={"batch": lax.rem(b + step, groups)},
            device_id_type=pl.DeviceIdType.MESH,
        )

    mark("b_route")
    route = r.route[...]
    row_id = lax.broadcasted_iota(jnp.int32, (slots, slots), 0)
    col_id = lax.broadcasted_iota(jnp.int32, (slots, slots), 1)
    route_col = jnp.sum(jnp.where(row_id == col_id, route, 0), axis=1, keepdims=True)
    token_id = lax.broadcasted_iota(jnp.int32, (slots, tokens), 1)
    pick = jnp.where(token_id == route_col, 1.0, 0.0).astype(bf16)
    count = jnp.sum(jnp.where(route >= 0, 1.0, 0.0), axis=1, keepdims=True)
    r.count_land[b] = jnp.broadcast_to(count, r.count_land.shape[1:])

    loads["student"].wait()
    r.x_land[0] = contract(pick, r.stud_v[...], 1, 0).astype(bf16)

    mark("c_barrier")
    pl.semaphore_wait(barrier, chips - 1 + 1 + groups - 1)

    mark("d_tprep")
    x_copies = [
        remote(
            r.x_land.at[0],
            r.x_land.at[step],
            r.x_sem.at[0, step],
            r.x_sem.at[1, step],
            tensor=2 * xor(chip, step, bits) + core,
        )
        for step in others
    ]
    for copy in x_copies[::-1]:
        copy.start()

    def count_copy(step):
        return remote(
            r.count_land.at[b],
            r.count_land.at[b],
            r.count_sem.at[0, step],
            r.count_sem.at[1, b],
            batch=lax.rem(b + step, groups),
        )

    for step in range(1, groups):
        count_copy(step).start()

    loads["attn"].wait()
    all_rows = slice(slots, slots + tokens)
    r.attn_v[0:slots] = contract(pick, r.attn_v[all_rows], 1, 0).astype(bf16)

    def pair_copy(send, land, sem, relative):
        return remote(
            send.at[relative],
            land.at[relative],
            sem.at[0, relative],
            sem.at[1, relative],
            tensor=partner,
        )

    piece = min(256, feats)

    def away(rows, send, land, sem, step):
        for place in range(0, feats, piece):
            span = slice(place, place + piece)
            value = jnp.dot(
                r.attn_v[rows], r.weight_v[step, :, span], preferred_element_type=f32
            )
            send[chips - 1 - step, :, span] = value.astype(bf16)
        pair_copy(send, land, sem, chips - 1 - step).start()

    def home(rows, send, land, sem, acc, step):
        relative = chips - 1 - step
        count = acc.shape[2]
        pair_copy(send, land, sem, relative).wait_recv()
        for place in range(0, feats, piece):
            span = slice(place, place + piece)
            value = jnp.dot(
                r.attn_v[rows], r.weight_v[chips + step, :, span], preferred_element_type=f32
            )
            value = (value + land[relative, :, span].astype(f32)).astype(bf16)
            for half in range(2):
                acc[relative, half, :, span] = value[half * count : (half + 1) * count]

    few = (slice(0, slots), r.q_send, r.q_land, r.q_sem)
    many = (all_rows, r.t_send, r.t_land, r.t_sem)
    routed_sum = PlaneScatter(
        r.r_acc, r.r_land, r.r_sem.at[0], r.r_sem.at[1], chip, core, bits
    )
    full_sum = PlaneScatter(
        r.f_acc, r.f_land, r.f_sem.at[0], r.f_sem.at[1], chip, core, bits
    )
    mark("e_away")
    for step in range(chips):
        loads[("w", step)].wait()
        away(*few, step)
    for step in range(chips):
        loads[("w", chips + step)].wait()
        home(*few, r.r_acc, step)
    routed_sum.send(0)

    mark("f_waitx")
    for copy in x_copies:
        copy.wait_recv()
    square = jnp.zeros((slots, 1), f32)
    for step in range(chips):
        value = r.x_land[step].astype(f32)
        square = square + jnp.sum(value * value, axis=1, keepdims=True)
    r.sq_send[...] = jnp.broadcast_to(square, r.sq_send.shape)
    sq_copy = remote(
        r.sq_send, r.sq_land, r.sq_sem.at[0], r.sq_sem.at[1], tensor=partner
    )
    sq_copy.start()
    away(*many, 0)
    away(*many, 1)
    mark("h_norm")
    sq_copy.wait_recv()
    square = r.sq_send[:, 0:1] + r.sq_land[:, 0:1]
    scale = lax.rsqrt(square / (width * tensors) + epsilon)

    def z_copy(relative, peer):
        return remote(
            r.z_send.at[relative],
            r.z_land.at[b],
            r.z_sem.at[0, relative],
            r.z_sem.at[1, b],
            batch=peer,
        )

    for relative in range(chips):
        peer = xor(chip, relative, bits)
        place = pl.multiple_of(peer * block + core * width, width)
        value = r.x_land[relative].astype(f32) * scale * r.gain[:, pl.ds(place, width)]
        value = value.astype(bf16)

        @pl.when(peer == b)
        def _():
            r.z_land[b] = value

        @pl.when(peer != b)
        def _():
            r.z_send[relative] = value
            z_copy(relative, peer).start()

    mark("i_home")
    for step in range(2, chips):
        away(*many, step)
    home(*many, r.f_acc, 0)
    mark("j_rrecv")
    routed_sum.receive(0)
    routed_sum.send(1)
    for stage in range(2, bits):
        routed_sum.receive(stage - 1)
        routed_sum.send(stage)
    mark("j2_home")
    for step in range(1, chips):
        home(*many, r.f_acc, step)

    mark("k_waitz")
    for group in range(groups):
        for land, sem in ((r.count_land, r.count_sem), (r.z_land, r.z_sem)):
            wait_recv_if(
                group != b,
                remote(
                    land.at[group], land.at[group], sem.at[0, 0], sem.at[1, group], batch=b
                ),
            )
    mark("l_pack")
    pack_row = lax.broadcasted_iota(jnp.int32, (routed, slots), 0).astype(f32)
    pack_col = lax.broadcasted_iota(jnp.int32, (routed, slots), 1).astype(f32)
    offset = jnp.zeros((1, 1), f32)
    packed = jnp.zeros((routed, width), f32)
    for group in range(groups):
        amount = r.count_land[group][0:1, 0:1]
        hit = jnp.logical_and(pack_col + offset == pack_row, pack_col < amount)
        r.select[group] = jnp.where(hit, 1.0, 0.0).astype(bf16)
        packed = packed + contract(r.select[group], r.z_land[group], 1, 0)
        offset = offset + amount
    r.rows_v[core] = packed.astype(bf16)
    row_copy = remote(
        r.rows_v.at[core], r.rows_v.at[core], r.row_sem.at[0], r.row_sem.at[1], tensor=partner
    )
    row_copy.start()

    mark("m_proj1")
    loads["w_gate"].wait()
    loads["w_up"].wait()

    def project(side, first):
        start = pl.multiple_of(side * width, width)
        rows = r.rows_v[side]
        for chunk in range(chunks):
            span = slice(chunk * cols, (chunk + 1) * cols)
            for which, weight in enumerate((r.wg, r.wu)):
                value = jnp.dot(
                    rows, weight[pl.ds(start, width), span], preferred_element_type=f32
                )
                for turn in range(2):
                    item = turn * chunks + chunk
                    piece = value[turn * tall : (turn + 1) * tall]
                    r.gu[item, which] = piece if first else r.gu[item, which] + piece

    project(core, True)
    mark("o_rowwait")
    remote(
        r.rows_v.at[1 - core],
        r.rows_v.at[1 - core],
        r.row_sem.at[0],
        r.row_sem.at[1],
        tensor=partner,
    ).wait_recv()
    mark("p_proj2")
    project(1 - core, False)
    gate_up = Chain(r.gu, r.gu_land, r.gu_share, r.gu_sem.at[0], r.gu_sem.at[1], b, groups)
    gate_up.origin(0, 2 * chunks)
    for side in range(2):
        r.o_rows[:, side * width : (side + 1) * width] = r.rows_v[side]

    mark("r_rrecv1")
    routed_sum.receive(bits - 1)
    loads["residual"].wait()
    routed_resid = contract(pick, r.resid_v[...], 1, 1)
    for half in range(2):
        first = half * (slots // 2)
        value = routed_sum.final(half) + routed_resid[first : first + slots // 2]
        r.p_keep[first : first + slots // 2] = value.astype(bf16)

    def target_copy(relative):
        return pair_copy(r.c_send, r.c_land, r.c_sem, relative)

    mark("s_target")
    for step in range(chips):
        relative = chips - 1 - step
        loads[("p", step)].wait()
        value = jnp.dot(r.p_keep[...], r.proj_v[step], preferred_element_type=f32)
        r.c_send[relative] = value.astype(bf16)
        target_copy(relative).start()
    target_sum = PlaneScatter(
        r.p_acc, r.p_land, r.p_sem.at[0], r.p_sem.at[1], chip, core, bits
    )

    def target_home():
        mark("u_target2")
        for step in range(chips):
            relative = chips - 1 - step
            loads[("p", chips + step)].wait()
            value = jnp.dot(r.p_keep[...], r.proj_v[chips + step], preferred_element_type=f32)
            target_copy(relative).wait_recv()
            value = (value + r.c_land[relative].astype(f32)).astype(bf16)
            for half in range(2):
                first = half * (slots // 2)
                r.p_acc[relative, half] = value[first : first + slots // 2]
        target_sum.send(0)

    def target_relay():
        mark("v_trelay")
        for stage in range(1, bits):
            target_sum.receive(stage - 1)
            target_sum.send(stage)
        full_sum.send(0)

    home_plane = chip == b

    def target_z(peer):
        return remote(
            r.p_send, r.p_zland.at[b], r.z2_sem.at[0], r.z2_sem.at[1 + b], batch=peer
        )

    def target_end():
        mark("x_tz")
        target_sum.receive(bits - 1)
        for half in range(2):
            first = half * (slots // 2)
            value = target_sum.final(half).astype(bf16)

            @pl.when(home_plane)
            def _():
                r.p_zland[b, first : first + slots // 2] = value

            @pl.when(jnp.logical_not(home_plane))
            def _():
                r.p_send[first : first + slots // 2] = value

        start_if(jnp.logical_not(home_plane), target_z(chip))

    def down(turn):
        mark(f"y_down{turn}")
        rows = slice(turn * tall, (turn + 1) * tall)
        if turn == 0:
            loads["w_down"].wait()
        for chunk in range(chunks):
            item = turn * chunks + chunk
            gate_up.total(item)
            gate, up = r.gu[item, 0], r.gu[item, 1]
            value = (gate * jax.nn.sigmoid(gate) * up).astype(bf16)
            r.o_hidden[rows, chunk * cols : (chunk + 1) * cols] = value
        r.part[turn] = contract(r.o_hidden[rows], r.wd[...], 1, 1)

        mark(f"z_tarrive{turn}")

        @pl.when(home_plane)
        def _():
            value = jnp.zeros((tall, width), f32)
            for group in range(groups):
                if turn == 0:
                    wait_recv_if(
                        group != b,
                        remote(
                            r.p_zland.at[group],
                            r.p_zland.at[group],
                            r.z2_sem.at[0],
                            r.z2_sem.at[1 + group],
                            batch=b,
                        ),
                    )
                value = value + contract(r.select[group, rows], r.p_zland[group], 1, 0)
            span = pl.ds(pl.multiple_of(core * width, width), width)
            r.part[turn, :, span] = r.part[turn, :, span] - value

    kept = pl.ds(pl.multiple_of(core * short, short), short)
    given = pl.ds(pl.multiple_of((1 - core) * short, short), short)
    half_cols = block // 2
    loss_scale = 1.0 / math.sqrt(routed)

    def misfit_copy(turn):
        return remote(
            r.m_send.at[turn],
            r.m_land.at[turn],
            r.m_sem.at[0, turn],
            r.m_sem.at[1, turn],
            tensor=partner,
        )

    def double_copy(turn, stage, half):
        bit = stage if half == 0 else bits - 1 - stage
        return remote(
            r.v_share.at[turn, stage, half],
            r.v_land.at[turn, stage, half],
            r.v_sem.at[0, turn, stage, half],
            r.v_sem.at[1, turn, stage, half],
            tensor=2 * xor(chip, 1 << bit, bits) + core,
        )

    def grad_copy(turn, side):
        return remote(
            r.grad_v.at[turn, side],
            r.grad_v.at[turn, side],
            r.g_sem.at[0, turn],
            r.g_sem.at[1, turn],
            tensor=partner,
        )

    def misfit_start(turn):
        mark(f"za_misfit{turn}")
        r.m_send[turn] = r.part[turn, given].astype(bf16)
        misfit_copy(turn).start()

    def double_start(turn, stage):
        mark(f"zb_dstart{turn}{stage}")
        if stage == 0:
            misfit_copy(turn).wait_recv()
            total = r.part[turn, kept] + r.m_land[turn].astype(f32)
            values = [total[:, :half_cols], total[:, half_cols:]]
        else:
            values = doubled(turn, stage - 1)
        for half in range(2):
            r.v_share[turn, stage, half] = values[half].astype(bf16)
            double_copy(turn, stage, half).start()

    def doubled(turn, stage):
        values = []
        for half in range(2):
            double_copy(turn, stage, half).wait_recv()
            values.append(
                r.v_share[turn, stage, half].astype(f32)
                + r.v_land[turn, stage, half].astype(f32)
            )
        return values

    def grad_start(turn):
        mark(f"zc_gstart{turn}")
        values = doubled(turn, bits - 1)
        for half in range(2):
            span = slice(half * half_cols, (half + 1) * half_cols)
            r.grad_v[turn, core, :, span] = (values[half] * loss_scale).astype(bf16)
        grad_copy(turn, core).start()

    grad_hidden = Chain(r.gh, r.gh_land, r.gh_share, r.gh_sem.at[0], r.gh_sem.at[1], b, groups)

    def back(turn):
        mark(f"zd_back{turn}")
        grad_copy(turn, 1 - core).wait_recv()
        for side in range(2):
            first = turn * tall + side * short
            r.o_grad[first : first + short] = r.grad_v[turn, side]
        rows = slice(turn * tall, (turn + 1) * tall)
        for chunk in range(chunks):
            span = slice(chunk * cols, (chunk + 1) * cols)
            r.gh[turn * chunks + chunk] = jnp.dot(
                r.o_grad[rows], r.wd[:, span], preferred_element_type=f32
            )
        grad_hidden.origin(turn * chunks, (turn + 1) * chunks)

    def last(turn):
        mark(f"zf_elem{turn}")
        rows = slice(turn * tall, (turn + 1) * tall)
        for chunk in range(chunks):
            item = turn * chunks + chunk
            grad_hidden.total(item)
            span = slice(chunk * cols, (chunk + 1) * cols)
            gate, up, grad = r.gu[item, 0], r.gu[item, 1], r.gh[item]
            sigma = jax.nn.sigmoid(gate)
            r.o_gate[rows, span] = (
                grad * up * sigma * (1.0 + gate * (1.0 - sigma))
            ).astype(bf16)
            r.o_up[rows, span] = (grad * gate * sigma).astype(bf16)

    def steps(chain, *items):
        for late, item in items:
            mark(f"chain{'gh' if chain is grad_hidden else 'gu'}{late}{item}")
            chain.step(item, bool(late))

    def both(chain, first, final, skew):
        for step in range(first, final + skew):
            if step < final:
                steps(chain, (0, step))
            if step - skew >= first:
                steps(chain, (1, step - skew))

    items = 2 * chunks
    skew = 2
    order = []
    for step in range(items + skew):
        if step < items:
            order.append((0, step))
        if step >= skew:
            order.append((1, step - skew))
    ready = order.index((1, chunks - 1)) + 1

    steps(gate_up, *order[:1])
    target_home()
    steps(gate_up, *order[1:4])
    target_relay()
    steps(gate_up, *order[4 : ready - 3])
    target_end()
    steps(gate_up, *order[ready - 3 : ready])
    down(0)
    misfit_start(0)
    rest = order[ready:]
    per = -(-len(rest) // (bits + 1))
    for stage in range(bits):
        steps(gate_up, *rest[stage * per : (stage + 1) * per])
        double_start(0, stage)
    steps(gate_up, *rest[bits * per : -1])
    grad_start(0)
    steps(gate_up, *rest[-1:])
    down(1)
    misfit_start(1)
    back(0)
    double_start(1, 0)
    order = []
    for step in range(chunks + skew):
        if step < chunks:
            order.append((0, step))
        if step >= skew:
            order.append((1, step - skew))
    steps(grad_hidden, *order[:2])
    for stage in range(1, bits):
        double_start(1, stage)
    steps(grad_hidden, *order[2:3])
    grad_start(1)
    steps(grad_hidden, *order[3:4])
    back(1)
    mark("zg_full0")
    for stage in range(1, bits):
        full_sum.receive(stage - 1)
        full_sum.send(stage)
    steps(grad_hidden, *order[4:])
    last(0)
    both(grad_hidden, chunks, items, skew)
    last(1)

    mark("zg_full")
    full_sum.receive(bits - 1)
    for half in range(2):
        span = slice(half * (tokens // 2), (half + 1) * (tokens // 2))
        value = full_sum.final(half).T + r.resid_v[:, span].astype(f32)
        r.o_teacher[:, span] = value.astype(bf16)

    mark("zh_drain")
    for copy in x_copies:
        copy.wait_send()
    for step in range(1, groups):
        count_copy(step).wait_send()
    for relative in range(chips):
        for send, land, sem in (few[1:], many[1:], (r.c_send, r.c_land, r.c_sem)):
            pair_copy(send, land, sem, relative).wait_send()
        peer = xor(chip, relative, bits)
        wait_send_if(peer != b, z_copy(relative, peer))
    wait_send_if(jnp.logical_not(home_plane), target_z(chip))
    sq_copy.wait_send()
    row_copy.wait_send()
    for turn in range(2):
        misfit_copy(turn).wait_send()
        grad_copy(turn, core).wait_send()
        for stage in range(bits):
            for half in range(2):
                double_copy(turn, stage, half).wait_send()
    routed_sum.drain()
    target_sum.drain()
    full_sum.drain()
    gate_up.drain()
    grad_hidden.drain()
    mark(None)


def grads_kernel(rows, gate, up, grad, hidden, teacher, o_gate, o_up, o_down, o_teacher):
    o_gate[...] = contract(rows[...], gate[...], 0, 0)
    o_up[...] = contract(rows[...], up[...], 0, 0)
    o_down[...] = contract(grad[...], hidden[...], 0, 0)
    o_teacher[...] = teacher[...]


def on_device(
    attn_values,
    out_weight,
    residual_t,
    projector,
    student_input,
    norm_gain,
    w_gate,
    w_up,
    w_down,
    route_index,
):
    groups, tensors = lax.axis_size("batch"), lax.axis_size("tensor")
    chips = tensors // 2
    bits = chips.bit_length() - 1
    if chips != groups or 1 << bits != chips:
        raise ValueError("mesh")
    mean_routed = student_input.shape[0] // 8
    routed = mean_routed * groups
    tokens, heads = attn_values.shape
    feats = out_weight.shape[1] // tensors
    model = projector.shape[1]
    width = student_input.shape[1]
    block, units = w_gate.shape
    slots = route_index.shape[1]
    cols = min(256, units)
    chunks = units // cols
    dma = pltpu.SemaphoreType.DMA
    moved = chips - 1
    scratch = [
        pltpu.VMEM((slots + tokens, heads), bf16),
        pltpu.VMEM((tensors, heads, feats), bf16),
        pltpu.VMEM(residual_t.shape, bf16),
        pltpu.VMEM((tensors, feats, width), bf16),
        pltpu.VMEM(student_input.shape, bf16),
        pltpu.VMEM(w_gate.shape, bf16),
        pltpu.VMEM(w_up.shape, bf16),
        pltpu.VMEM(w_down.shape, bf16),
        dma((6 + 2 * tensors,)),
        pltpu.VMEM((chips, slots, feats), bf16),
        pltpu.VMEM((chips, slots, feats), bf16),
        dma((2, chips)),
        pltpu.VMEM((chips, tokens, feats), bf16),
        pltpu.VMEM((chips, tokens, feats), bf16),
        pltpu.VMEM((chips, 2, slots // 2, feats), bf16),
        pltpu.VMEM((moved, 2, slots // 2, feats), bf16),
        pltpu.VMEM((chips, 2, tokens // 2, feats), bf16),
        pltpu.VMEM((moved, 2, tokens // 2, feats), bf16),
        dma((2, chips)),
        dma((2, moved, 2)),
        dma((2, moved, 2)),
        pltpu.VMEM((chips, slots, width), bf16),
        pltpu.VMEM((chips, slots, width), bf16),
        pltpu.VMEM((chips, 2, slots // 2, width), bf16),
        pltpu.VMEM((moved, 2, slots // 2, width), bf16),
        pltpu.VMEM((slots, feats), bf16),
        pltpu.VMEM((slots, width), bf16),
        pltpu.VMEM((groups, slots, width), bf16),
        dma((2, chips)),
        dma((2, moved, 2)),
        dma((1 + groups,)),
        pltpu.VMEM((chips, slots, width), bf16),
        pltpu.VMEM((slots, 128), f32),
        pltpu.VMEM((slots, 128), f32),
        pltpu.VMEM((groups, 8, 128), f32),
        dma((2, chips)),
        dma((2,)),
        dma((2, groups)),
        pltpu.VMEM((chips, slots, width), bf16),
        pltpu.VMEM((groups, slots, width), bf16),
        dma((2, max(chips, groups))),
        pltpu.VMEM((groups, routed, slots), bf16),
        pltpu.VMEM((2, routed, width), bf16),
        dma((2,)),
        pltpu.VMEM((2 * chunks, 2, routed // 2, cols), f32),
        pltpu.VMEM((2, 2 * chunks, 2, routed // 2, cols), bf16),
        pltpu.VMEM((2, 2 * chunks, 2, routed // 2, cols), bf16),
        dma((2, 2, 2 * chunks)),
        pltpu.VMEM((2 * chunks, routed // 2, cols), f32),
        pltpu.VMEM((2, 2 * chunks, routed // 2, cols), bf16),
        pltpu.VMEM((2, 2 * chunks, routed // 2, cols), bf16),
        dma((2, 2, 2 * chunks)),
        pltpu.VMEM((2, routed // 2, block), f32),
        pltpu.VMEM((2, routed // 4, block), bf16),
        pltpu.VMEM((2, routed // 4, block), bf16),
        pltpu.VMEM((2, bits, 2, routed // 4, block // 2), bf16),
        pltpu.VMEM((2, bits, 2, routed // 4, block // 2), bf16),
        dma((2, 2)),
        dma((2, 2, bits, 2)),
        pltpu.VMEM((2, 2, routed // 4, block), bf16),
        dma((2, 2)),
    ]
    rows, gate, up, grad, hidden, teacher = pl.pallas_call(
        functools.partial(exchange_kernel, (groups, tensors, mean_routed)),
        name="exchange",
        out_shape=(
            jax.ShapeDtypeStruct((routed, block), bf16),
            jax.ShapeDtypeStruct((routed, units), bf16),
            jax.ShapeDtypeStruct((routed, units), bf16),
            jax.ShapeDtypeStruct((routed, block), bf16),
            jax.ShapeDtypeStruct((routed, units), bf16),
            jax.ShapeDtypeStruct(residual_t.shape, bf16),
        ),
        in_specs=[ANY, ANY, ANY, ANY, ANY, VMEM, ANY, ANY, ANY, VMEM],
        out_specs=[VMEM] * 6,
        scratch_shapes=scratch,
        compiler_params=pltpu.CompilerParams(
            collective_id=1, has_side_effects=True, vmem_limit_bytes=VMEM_BYTES
        ),
    )(
        attn_values,
        out_weight,
        residual_t,
        projector,
        student_input,
        norm_gain.reshape(1, -1),
        w_gate,
        w_up,
        w_down,
        route_index,
    )
    parts = 4
    tall = block // parts
    high = residual_t.shape[0] // parts
    whole = lambda array: pl.BlockSpec(array.shape, lambda i: (0, 0))
    strip = pl.BlockSpec((routed, tall), lambda i: (0, i))
    out = pl.BlockSpec((tall, units), lambda i: (i, 0))
    flat = pl.BlockSpec((high, residual_t.shape[1]), lambda i: (i, 0))
    grads = jax.ShapeDtypeStruct((block, units), f32)
    grad_gate, grad_up, grad_down, teacher_hidden = pl.pallas_call(
        grads_kernel,
        name="grads",
        grid=(parts,),
        out_shape=(grads, grads, grads, jax.ShapeDtypeStruct(residual_t.shape, bf16)),
        in_specs=[strip, whole(gate), whole(up), strip, whole(hidden), flat],
        out_specs=[out, out, out, flat],
    )(rows, gate, up, grad, hidden, teacher)
    return (teacher_hidden, grad_gate, grad_up, grad_down)


def solution(mesh):
    in_specs = (
        P("batch", "tensor"),
        P("tensor", None),
        P("tensor", "batch"),
        P("tensor", None),
        P("batch", "tensor"),
        P(),
        P("batch", "tensor"),
        P("batch", "tensor"),
        P("batch", "tensor"),
        P("batch", None),
    )
    out_specs = (
        P("tensor", "batch"),
        P("batch", "tensor"),
        P("batch", "tensor"),
        P("batch", "tensor"),
    )
    return jax.shard_map(
        on_device, mesh=mesh, in_specs=in_specs, out_specs=out_specs, check_vma=False
    )
```

time: 186 us -> 85.4 us (0.46)
  matrix products: 38.3 us -> 0 us
  Pallas kernels: 112 us -> 84.5 us
  between operations: 14.3 us -> 0.64 us
  other arithmetic: 10.6 us -> 0 us
  local copies, waits for them, and re-layouts: 9.86 us -> 0 us
    dot_general x11 -> x0, matrix products: 38.3 us -> none  [contract(): lax.dot_general(left, right, (((left_dim,), (right_dim,)), ((), ())), pre...]
    pallas_call x7 -> x2, Pallas kernels: 112 us -> 84.5 us  [the longest x1 78 us: on_device(): pl.pallas_call(functools.partial(exchange_kernel, (groups, tensors, mean_...]
    convert_element_type x4 -> x0, other arithmetic: 4.09 us -> none  [the longest x1 1.96 us: on_device(): teacher_hidden = (residual_t.astype(f32) + summed).astype(bf16)]
    unnamed x22 -> x0, local copies, waits for them, and re-layouts: 2.15 us -> none
    reshape x3 -> x0, local copies, waits for them, and re-layouts: 2.12 us -> none  [the longest x2 1.29 us: on_device(): jnp.swapaxes(normed, 0, 1).reshape(slot_pos.shape[0], group_count, -1)]
  transfers between devices with their start and end apart: 1 -> 0, of which waited for: 0 -> 0; matrix products, arithmetic and copies ran while one was open for 11% -> 0% of each run, Pallas kernels for 34% -> 0%
where the time goes in v1:
time: 85.4 us; the launch traced here: 85.1 us
  Pallas kernels  84.5 us (99%)
    pallas_call x1, Pallas kernels, on_device(): pl.pallas_call(functools.partial(exchange_kernel, (groups, tensors, mean_...  78 us
    pallas_call x1, Pallas kernels, on_device(): pl.pallas_call(grads_kernel, name='grads', grid=(parts,), out_shape=(grad...  6.54 us

profile of v1, /device:TPU:0, one launch (start us, length us, event | category | flops | bytes accessed | tf_op | source)
XLA Modules:
  0.0 85.1 jit_solution(18089614574971715214)
XLA Ops:
  0.6 78.0 %exchange.1 = (bf16[128,1024]{1,0:T(8,128)(2,1)}, bf16[128,1024]{1,0:T(8,128)(2,1)}, bf16[128,1024]{1,0:T(8,128)(2,1)}, bf16[128,1024]{1,0:T(8,128)(2,1)}, bf16[...) custom-call(bf16[256,1024]{1,0:T(8,128)(2,1)} %refs_0_.1, bf16[1024,8192]{1,0:T(8,128)(2,1)} %refs_1_.1, ...), custom_call_target="tpu_custom_call" | custom-call | tf_op jit(solution)/shard_map/exchange/pallas_call | solution.py:904
  78.6 6.5 %grads.1 = (f32[1024,1024]{1,0:T(8,128)}, f32[1024,1024]{1,0:T(8,128)}, f32[1024,1024]{1,0:T(8,128)}, bf16[1024,256]{1,0:T(8,128)(2,1)}) custom-call(bf16[128,1024]{1,0:T(8,128)(2,1)} %get-tuple-element.14.rows, bf16[128,1024]{1,0:T(8,128)(2,1)} %get-tuple-element.15.gate, bf16[128,1024]{1,0:T(8,128)(2,1)} %get-tuple-element.16.up, ...), custom_call_target="tpu_custom_call" | custom-call | tf_op jit(solution)/shard_map/grads/pallas_call | solution.py:941

commit v2 on v1

--- a/solution.py
+++ b/solution.py
@@ -13,13 +13,14 @@
 f32 = jnp.float32
 bf16 = jnp.bfloat16
 VMEM = pl.BlockSpec(memory_space=pltpu.VMEM)
-ANY = pl.BlockSpec(memory_space=pl.ANY)
-VMEM_BYTES = 66_000_000
+HBM = pl.BlockSpec(memory_space=pltpu.HBM)
+VMEM_BYTES = 54_000_000
 
 NAMES = (
     "attn", "out_weight", "residual", "projector", "student", "gain", "w_gate", "w_up",
     "w_down", "route", "o_rows", "o_gate", "o_up", "o_grad", "o_hidden", "o_teacher",
-    "attn_v", "weight_v", "resid_v", "proj_v", "stud_v", "wg", "wu", "wd", "load_sem",
+    "attn_v", "weight_v", "resid_v", "proj_v", "stud_v", "wg", "wu", "wd", "route_v", "gain_v",
+    "load_sem",
     "q_send", "q_land", "q_sem", "t_send", "t_land", "r_acc", "r_land", "f_acc", "f_land", "t_sem", "r_sem", "f_sem",
     "c_send", "c_land", "p_acc", "p_land", "p_keep", "p_send", "p_zland", "c_sem", "p_sem", "z2_sem",
     "x_land", "sq_send", "sq_land", "count_land", "x_sem", "sq_sem", "count_sem", "z_send",
@@ -120,16 +121,21 @@
     def step(self, chunk, late):
         way, before, after, peer = self.flow(late)
         copy = self.copy(way, chunk, peer)
-        wait_recv_if(before, copy)
 
         @pl.when(jnp.logical_and(after, before))
         def _():
+            copy.wait_recv()
             self.share[way, chunk] = (
                 self.own[chunk] + self.land[way, chunk].astype(f32)
             ).astype(bf16)
             copy.start()
 
     def total(self, chunk):
+        way, before, after, peer = self.flow(True)
+        wait_recv_if(
+            jnp.logical_and(before, jnp.logical_not(after)), self.copy(way, chunk, peer)
+        )
+
         @pl.when(self.me > 0)
         def _():
             self.own[chunk] = self.own[chunk] + self.land[0, chunk].astype(f32)
@@ -146,8 +152,8 @@
 
 
 class PlaneScatter:
-    def __init__(self, acc, land, send_sem, recv_sem, chip, core, bits):
-        self.acc, self.land = acc, land
+    def __init__(self, acc, land, send_sem, recv_sem, chip, core, bits, absolute=False):
+        self.acc, self.land, self.absolute = acc, land, absolute
         self.send_sem, self.recv_sem = send_sem, recv_sem
         self.chip, self.core, self.bits = chip, core, bits
         self.slots, self.stages = [], []
@@ -170,11 +176,14 @@
             self.slots.append(slots)
             self.stages.append(stages)
 
+    def place(self, block):
+        return xor(self.chip, block, self.bits) if self.absolute else block
+
     def copy(self, half, stage, block):
         flip, _ = self.stages[half][stage]
         slot = self.slots[half][(stage, block ^ flip)]
         return remote(
-            self.acc.at[block, half],
+            self.acc.at[self.place(block), half],
             self.land.at[slot, half],
             self.send_sem.at[slot, half],
             self.recv_sem.at[slot, half],
@@ -187,14 +196,15 @@
             for stage in range(stages)
         ]
 
-    def send(self, stage):
+    def send(self, stage, first=0, last=None):
         for half in range(2):
-            for block in self.stages[half][stage][1]:
+            for block in self.stages[half][stage][1][first:last]:
+                place = self.place(block)
                 if stage:
-                    value = self.acc[block, half].astype(f32)
+                    value = self.acc[place, half].astype(f32)
                     for term in self.arrived(half, stage, block):
                         value = value + term
-                    self.acc[block, half] = value.astype(bf16)
+                    self.acc[place, half] = value.astype(bf16)
                 self.copy(half, stage, block).start()
 
     def receive(self, stage):
@@ -203,7 +213,7 @@
                 self.copy(half, stage, block).wait_recv()
 
     def final(self, half):
-        value = self.acc[0, half].astype(f32)
+        value = self.acc[self.place(0), half].astype(f32)
         for term in self.arrived(half, self.bits, 0):
             value = value + term
         return value
@@ -235,6 +245,7 @@
     short = routed // 4
     chunks = r.gu.shape[0] // 2
     cols = hidden_units // chunks
+    portion = slots // chips
     others = range(1, chips)
 
     mark("a_loads")
@@ -252,6 +263,7 @@
     def owner(relative, side):
         return 2 * xor(chip, relative, bits) + (core if side else 1 - core)
 
+    load("route", r.route, r.route_v)
     load("student", r.student, r.stud_v)
     load("attn", r.attn, r.attn_v.at[pl.ds(slots, tokens)])
     for side in range(2):
@@ -259,12 +271,14 @@
             place = side * chips + step
             index = owner(chips - 1 - step, side)
             load(("w", place), weight_block(index), r.weight_v.at[place])
+    load("gain", r.gain, r.gain_v)
     load("w_gate", r.w_gate, r.wg)
     load("w_up", r.w_up, r.wu)
     load("residual", r.residual, r.resid_v)
     for side in range(2):
         for step in range(chips):
-            place = pl.multiple_of(owner(chips - 1 - step, side) * width, width)
+            index = 2 * step + (core if side else 1 - core)
+            place = pl.multiple_of(index * width, width)
             load(
                 ("p", side * chips + step),
                 r.projector.at[:, pl.ds(place, width)],
@@ -292,7 +306,8 @@
         )
 
     mark("b_route")
-    route = r.route[...]
+    loads["route"].wait()
+    route = r.route_v[...]
     row_id = lax.broadcasted_iota(jnp.int32, (slots, slots), 0)
     col_id = lax.broadcasted_iota(jnp.int32, (slots, slots), 1)
     route_col = jnp.sum(jnp.where(row_id == col_id, route, 0), axis=1, keepdims=True)
@@ -400,10 +415,10 @@
     )
     sq_copy.start()
     away(*many, 0)
-    away(*many, 1)
     mark("h_norm")
     sq_copy.wait_recv()
     square = r.sq_send[:, 0:1] + r.sq_land[:, 0:1]
+    loads["gain"].wait()
     scale = lax.rsqrt(square / (width * tensors) + epsilon)
 
     def z_copy(relative, peer):
@@ -418,7 +433,7 @@
     for relative in range(chips):
         peer = xor(chip, relative, bits)
         place = pl.multiple_of(peer * block + core * width, width)
-        value = r.x_land[relative].astype(f32) * scale * r.gain[:, pl.ds(place, width)]
+        value = r.x_land[relative].astype(f32) * scale * r.gain_v[:, pl.ds(place, width)]
         value = value.astype(bf16)
 
         @pl.when(peer == b)
@@ -431,7 +446,7 @@
             z_copy(relative, peer).start()
 
     mark("i_home")
-    for step in range(2, chips):
+    for step in range(1, chips):
         away(*many, step)
     home(*many, r.f_acc, 0)
     mark("j_rrecv")
@@ -440,6 +455,7 @@
     for stage in range(2, bits):
         routed_sum.receive(stage - 1)
         routed_sum.send(stage)
+    full_sum.send(0, 0, 1)
     mark("j2_home")
     for step in range(1, chips):
         home(*many, r.f_acc, step)
@@ -456,13 +472,17 @@
     mark("l_pack")
     pack_row = lax.broadcasted_iota(jnp.int32, (routed, slots), 0).astype(f32)
     pack_col = lax.broadcasted_iota(jnp.int32, (routed, slots), 1).astype(f32)
+    mine_row = lax.broadcasted_iota(jnp.int32, (routed, portion), 0).astype(f32)
+    mine_col = lax.broadcasted_iota(jnp.int32, (routed, portion), 1) + chip * portion
+    mine_col = mine_col.astype(f32)
     offset = jnp.zeros((1, 1), f32)
     packed = jnp.zeros((routed, width), f32)
     for group in range(groups):
         amount = r.count_land[group][0:1, 0:1]
         hit = jnp.logical_and(pack_col + offset == pack_row, pack_col < amount)
+        packed = packed + contract(jnp.where(hit, 1.0, 0.0).astype(bf16), r.z_land[group], 1, 0)
+        hit = jnp.logical_and(mine_col + offset == mine_row, mine_col < amount)
         r.select[group] = jnp.where(hit, 1.0, 0.0).astype(bf16)
-        packed = packed + contract(r.select[group], r.z_land[group], 1, 0)
         offset = offset + amount
     r.rows_v[core] = packed.astype(bf16)
     row_copy = remote(
@@ -500,7 +520,7 @@
     mark("p_proj2")
     project(1 - core, False)
     gate_up = Chain(r.gu, r.gu_land, r.gu_share, r.gu_sem.at[0], r.gu_sem.at[1], b, groups)
-    gate_up.origin(0, 2 * chunks)
+    gate_up.origin(0, chunks)
     for side in range(2):
         r.o_rows[:, side * width : (side + 1) * width] = r.rows_v[side]
 
@@ -517,27 +537,27 @@
         return pair_copy(r.c_send, r.c_land, r.c_sem, relative)
 
     mark("s_target")
-    for step in range(chips):
-        relative = chips - 1 - step
+    for step in range(groups):
         loads[("p", step)].wait()
         value = jnp.dot(r.p_keep[...], r.proj_v[step], preferred_element_type=f32)
-        r.c_send[relative] = value.astype(bf16)
-        target_copy(relative).start()
+        r.c_send[step] = value.astype(bf16)
+        target_copy(step).start()
     target_sum = PlaneScatter(
-        r.p_acc, r.p_land, r.p_sem.at[0], r.p_sem.at[1], chip, core, bits
-    )
+        r.p_acc, r.p_land, r.p_sem.at[0], r.p_sem.at[1], chip, core, bits, absolute=True
+    )
+    side_blocks = groups // 2
 
     def target_home():
         mark("u_target2")
-        for step in range(chips):
-            relative = chips - 1 - step
-            loads[("p", chips + step)].wait()
-            value = jnp.dot(r.p_keep[...], r.proj_v[chips + step], preferred_element_type=f32)
-            target_copy(relative).wait_recv()
-            value = (value + r.c_land[relative].astype(f32)).astype(bf16)
-            for half in range(2):
-                first = half * (slots // 2)
-                r.p_acc[relative, half] = value[first : first + slots // 2]
+        for step in range(groups):
+            loads[("p", groups + step)].wait()
+            value = jnp.dot(r.p_keep[...], r.proj_v[groups + step], preferred_element_type=f32)
+            target_copy(step).wait_recv()
+            value = (value + r.c_land[step].astype(f32)).astype(bf16)
+            half, place = step // side_blocks, step % side_blocks * width
+            for owner in range(chips):
+                rows = value[owner * portion : (owner + 1) * portion]
+                r.p_acc[owner, half, :, place : place + width] = rows
         target_sum.send(0)
 
     def target_relay():
@@ -545,31 +565,35 @@
         for stage in range(1, bits):
             target_sum.receive(stage - 1)
             target_sum.send(stage)
-        full_sum.send(0)
-
-    home_plane = chip == b
 
     def target_z(peer):
         return remote(
-            r.p_send, r.p_zland.at[b], r.z2_sem.at[0], r.z2_sem.at[1 + b], batch=peer
+            r.p_send.at[peer],
+            r.p_zland.at[b],
+            r.z2_sem.at[0, peer],
+            r.z2_sem.at[1, b],
+            batch=peer,
         )
 
     def target_end():
         mark("x_tz")
         target_sum.receive(bits - 1)
         for half in range(2):
-            first = half * (slots // 2)
             value = target_sum.final(half).astype(bf16)
-
-            @pl.when(home_plane)
-            def _():
-                r.p_zland[b, first : first + slots // 2] = value
-
-            @pl.when(jnp.logical_not(home_plane))
-            def _():
-                r.p_send[first : first + slots // 2] = value
-
-        start_if(jnp.logical_not(home_plane), target_z(chip))
+            for place in range(side_blocks):
+                peer = half * side_blocks + place
+                part = value[:, place * width : (place + 1) * width]
+
+                @pl.when(peer == b)
+                def _():
+                    r.p_zland[b] = part
+
+                @pl.when(peer != b)
+                def _():
+                    r.p_send[peer] = part
+                    target_z(peer).start()
+
+        full_sum.send(0, 1)
 
     def down(turn):
         mark(f"y_down{turn}")
@@ -585,25 +609,22 @@
         r.part[turn] = contract(r.o_hidden[rows], r.wd[...], 1, 1)
 
         mark(f"z_tarrive{turn}")
-
-        @pl.when(home_plane)
-        def _():
-            value = jnp.zeros((tall, width), f32)
-            for group in range(groups):
-                if turn == 0:
-                    wait_recv_if(
-                        group != b,
-                        remote(
-                            r.p_zland.at[group],
-                            r.p_zland.at[group],
-                            r.z2_sem.at[0],
-                            r.z2_sem.at[1 + group],
-                            batch=b,
-                        ),
-                    )
-                value = value + contract(r.select[group, rows], r.p_zland[group], 1, 0)
-            span = pl.ds(pl.multiple_of(core * width, width), width)
-            r.part[turn, :, span] = r.part[turn, :, span] - value
+        value = jnp.zeros((tall, width), f32)
+        for group in range(groups):
+            if turn == 0:
+                wait_recv_if(
+                    group != b,
+                    remote(
+                        r.p_zland.at[group],
+                        r.p_zland.at[group],
+                        r.z2_sem.at[0, 0],
+                        r.z2_sem.at[1, group],
+                        batch=b,
+                    ),
+                )
+            value = value + contract(r.select[group, rows], r.p_zland[group], 1, 0)
+        span = pl.ds(pl.multiple_of(core * width, width), width)
+        r.part[turn, :, span] = r.part[turn, :, span] - value
 
     kept = pl.ds(pl.multiple_of(core * short, short), short)
     given = pl.ds(pl.multiple_of((1 - core) * short, short), short)
@@ -708,64 +729,57 @@
             mark(f"chain{'gh' if chain is grad_hidden else 'gu'}{late}{item}")
             chain.step(item, bool(late))
 
-    def both(chain, first, final, skew):
+    def order_of(first, final, skew):
+        order = []
         for step in range(first, final + skew):
             if step < final:
-                steps(chain, (0, step))
+                order.append((0, step))
             if step - skew >= first:
-                steps(chain, (1, step - skew))
+                order.append((1, step - skew))
+        return order
 
     items = 2 * chunks
-    skew = 2
-    order = []
-    for step in range(items + skew):
-        if step < items:
-            order.append((0, step))
-        if step >= skew:
-            order.append((1, step - skew))
-    ready = order.index((1, chunks - 1)) + 1
-
-    steps(gate_up, *order[:1])
+    order = order_of(0, items, min(5, chunks))
+    late = [order.index((1, item)) + 1 for item in range(items)]
+
     target_home()
-    steps(gate_up, *order[1:4])
+    gate_up.origin(chunks, items)
+    steps(gate_up, *order[: late[0] - 3])
     target_relay()
-    steps(gate_up, *order[4 : ready - 3])
+    steps(gate_up, *order[late[0] - 3 : late[chunks - 3]])
     target_end()
-    steps(gate_up, *order[ready - 3 : ready])
+    begin = min(items - 2, chunks + 1)
+    steps(gate_up, *order[late[chunks - 3] : late[begin]])
     down(0)
     misfit_start(0)
-    rest = order[ready:]
-    per = -(-len(rest) // (bits + 1))
     for stage in range(bits):
-        steps(gate_up, *rest[stage * per : (stage + 1) * per])
+        end = min(items - 1, begin + 2)
+        steps(gate_up, *order[late[begin] : late[end]])
         double_start(0, stage)
-    steps(gate_up, *rest[bits * per : -1])
-    grad_start(0)
-    steps(gate_up, *rest[-1:])
+        begin = end
+    steps(gate_up, *order[late[begin] :])
     down(1)
     misfit_start(1)
+    grad_start(0)
+    double_start(1, 0)
     back(0)
-    double_start(1, 0)
-    order = []
-    for step in range(chunks + skew):
-        if step < chunks:
-            order.append((0, step))
-        if step >= skew:
-            order.append((1, step - skew))
+
+    order = order_of(0, chunks, chunks)
+    late = [order.index((1, item)) + 1 for item in range(chunks)]
     steps(grad_hidden, *order[:2])
     for stage in range(1, bits):
         double_start(1, stage)
-    steps(grad_hidden, *order[2:3])
+    steps(grad_hidden, *order[2 : late[0] - 1])
     grad_start(1)
-    steps(grad_hidden, *order[3:4])
+    steps(grad_hidden, *order[late[0] - 1 : late[3]])
     back(1)
     mark("zg_full0")
     for stage in range(1, bits):
         full_sum.receive(stage - 1)
         full_sum.send(stage)
-    steps(grad_hidden, *order[4:])
+    steps(grad_hidden, *order[late[3] :])
     last(0)
-    both(grad_hidden, chunks, items, skew)
+    steps(grad_hidden, *order_of(chunks, items, chunks))
     last(1)
 
     mark("zg_full")
@@ -785,7 +799,8 @@
             pair_copy(send, land, sem, relative).wait_send()
         peer = xor(chip, relative, bits)
         wait_send_if(peer != b, z_copy(relative, peer))
-    wait_send_if(jnp.logical_not(home_plane), target_z(chip))
+    for peer in range(groups):
+        wait_send_if(peer != b, target_z(peer))
     sq_copy.wait_send()
     row_copy.wait_send()
     for turn in range(2):
@@ -802,11 +817,22 @@
     mark(None)
 
 
-def grads_kernel(rows, gate, up, grad, hidden, teacher, o_gate, o_up, o_down, o_teacher):
-    o_gate[...] = contract(rows[...], gate[...], 0, 0)
-    o_up[...] = contract(rows[...], up[...], 0, 0)
-    o_down[...] = contract(grad[...], hidden[...], 0, 0)
-    o_teacher[...] = teacher[...]
+def grads_kernel(
+    rows, gate, up, grad, hidden, teacher, o_gate, o_up, o_down, o_teacher, hold, sem, end_sem
+):
+    count, parts, tall, _ = hold.shape
+    copies = [pltpu.make_async_copy(teacher, o_teacher, end_sem.at[0])]
+    copies[0].start()
+    terms = ((grad, hidden, o_down), (rows, gate, o_gate), (rows, up, o_up))
+    for which, (left, right, out) in enumerate(terms):
+        for part in range(parts):
+            span = pl.ds(part * tall, tall)
+            hold[which, part] = contract(left[:, span], right[...], 0, 0)
+            copy = pltpu.make_async_copy(hold.at[which, part], out.at[span], sem.at[which, part])
+            copy.start()
+            copies.append(copy)
+    for copy in copies:
+        copy.wait()
 
 
 def on_device(
@@ -834,7 +860,7 @@
     width = student_input.shape[1]
     block, units = w_gate.shape
     slots = route_index.shape[1]
-    cols = min(256, units)
+    cols = min(128, units)
     chunks = units // cols
     dma = pltpu.SemaphoreType.DMA
     moved = chips - 1
@@ -847,7 +873,9 @@
         pltpu.VMEM(w_gate.shape, bf16),
         pltpu.VMEM(w_up.shape, bf16),
         pltpu.VMEM(w_down.shape, bf16),
-        dma((6 + 2 * tensors,)),
+        pltpu.VMEM(route_index.shape, route_index.dtype),
+        pltpu.VMEM((1, model), f32),
+        dma((8 + 2 * tensors,)),
         pltpu.VMEM((chips, slots, feats), bf16),
         pltpu.VMEM((chips, slots, feats), bf16),
         dma((2, chips)),
@@ -862,14 +890,14 @@
         dma((2, moved, 2)),
         pltpu.VMEM((chips, slots, width), bf16),
         pltpu.VMEM((chips, slots, width), bf16),
-        pltpu.VMEM((chips, 2, slots // 2, width), bf16),
-        pltpu.VMEM((moved, 2, slots // 2, width), bf16),
+        pltpu.VMEM((chips, 2, slots // chips, model // 4), bf16),
+        pltpu.VMEM((moved, 2, slots // chips, model // 4), bf16),
         pltpu.VMEM((slots, feats), bf16),
-        pltpu.VMEM((slots, width), bf16),
-        pltpu.VMEM((groups, slots, width), bf16),
+        pltpu.VMEM((groups, slots // chips, width), bf16),
+        pltpu.VMEM((groups, slots // chips, width), bf16),
         dma((2, chips)),
         dma((2, moved, 2)),
-        dma((1 + groups,)),
+        dma((2, groups)),
         pltpu.VMEM((chips, slots, width), bf16),
         pltpu.VMEM((slots, 128), f32),
         pltpu.VMEM((slots, 128), f32),
@@ -880,7 +908,7 @@
         pltpu.VMEM((chips, slots, width), bf16),
         pltpu.VMEM((groups, slots, width), bf16),
         dma((2, max(chips, groups))),
-        pltpu.VMEM((groups, routed, slots), bf16),
+        pltpu.VMEM((groups, routed, slots // chips), bf16),
         pltpu.VMEM((2, routed, width), bf16),
         dma((2,)),
         pltpu.VMEM((2 * chunks, 2, routed // 2, cols), f32),
@@ -912,7 +940,7 @@
             jax.ShapeDtypeStruct((routed, units), bf16),
             jax.ShapeDtypeStruct(residual_t.shape, bf16),
         ),
-        in_specs=[ANY, ANY, ANY, ANY, ANY, VMEM, ANY, ANY, ANY, VMEM],
+        in_specs=[HBM] * 10,
         out_specs=[VMEM] * 6,
         scratch_shapes=scratch,
         compiler_params=pltpu.CompilerParams(
@@ -931,20 +959,19 @@
         route_index,
     )
     parts = 4
-    tall = block // parts
-    high = residual_t.shape[0] // parts
-    whole = lambda array: pl.BlockSpec(array.shape, lambda i: (0, 0))
-    strip = pl.BlockSpec((routed, tall), lambda i: (0, i))
-    out = pl.BlockSpec((tall, units), lambda i: (i, 0))
-    flat = pl.BlockSpec((high, residual_t.shape[1]), lambda i: (i, 0))
     grads = jax.ShapeDtypeStruct((block, units), f32)
     grad_gate, grad_up, grad_down, teacher_hidden = pl.pallas_call(
         grads_kernel,
         name="grads",
-        grid=(parts,),
         out_shape=(grads, grads, grads, jax.ShapeDtypeStruct(residual_t.shape, bf16)),
-        in_specs=[strip, whole(gate), whole(up), strip, whole(hidden), flat],
-        out_specs=[out, out, out, flat],
+        in_specs=[VMEM] * 6,
+        out_specs=[HBM] * 4,
+        scratch_shapes=[
+            pltpu.VMEM((3, parts, block // parts, units), f32),
+            dma((3, parts)),
+            dma((1,)),
+        ],
+        compiler_params=pltpu.CompilerParams(vmem_limit_bytes=20_000_000),
     )(rows, gate, up, grad, hidden, teacher)
     return (teacher_hidden, grad_gate, grad_up, grad_down)
 

time: 85.4 us -> 73.6 us (0.86)
  Pallas kernels: 84.5 us -> 70.3 us
  local copies, waits for them, and re-layouts: 0 us -> 2.31 us
    pallas_call x1, Pallas kernels: 78 us -> 65.1 us  [on_device(): pl.pallas_call(functools.partial(exchange_kernel, (groups, tensors, mean_...]
    unnamed x0 -> x6, local copies, waits for them, and re-layouts: none -> 2.31 us
    pallas_call x1, Pallas kernels: 6.54 us -> 5.15 us  [on_device(): pl.pallas_call(grads_kernel, name='grads', out_shape=(grads, grads, grads...]
where the time goes in v2:
time: 73.6 us; the launch traced here: 73.4 us
  Pallas kernels  70.3 us (96%)
  local copies, waits for them, and re-layouts  2.31 us (3%)
  between operations  0.81 us (1%)
    pallas_call x1, Pallas kernels, on_device(): pl.pallas_call(functools.partial(exchange_kernel, (groups, tensors, mean_...  65.1 us
    pallas_call x1, Pallas kernels, on_device(): pl.pallas_call(grads_kernel, name='grads', out_shape=(grads, grads, grads...  5.15 us
    unnamed x6, local copies, waits for them, and re-layouts  2.31 us

profile of v2, /device:TPU:0, one launch (start us, length us, event | category | flops | bytes accessed | tf_op | source)
XLA Modules:
  0.0 73.4 jit_solution(1023344822603543075)
XLA Ops:
  0.6 0.0 copy-start
  0.6 0.9 %copy-done = bf16[256,512]{1,0:T(8,128)(2,1)S(1)} copy-done((bf16[256,512]{1,0:T(8,128)(2,1)S(1)}, bf16[256,512]{1,0:T(8,128)(2,1)}, u32[]{:S(2)}) %copy-start) | copy-done | bytes 262168
  1.6 0.0 copy-start.1
  1.6 0.7 copy-done.1
  2.3 0.0 copy-start.2
  2.3 0.7 copy-done.2
  3.0 65.1 %exchange.1 = (bf16[128,1024]{1,0:T(8,128)(2,1)S(1)}, bf16[128,1024]{1,0:T(8,128)(2,1)S(1)}, bf16[128,1024]{1,0:T(8,128)(2,1)S(1)}, bf16[128,1024]{1,0:T(8,128)(...) custom-call(bf16[256,1024]{1,0:T(8,128)(2,1)} %refs_0_.1, bf16[1024,8192]{1,0:T(8,128)(2,1)} %refs_1_.1, ...), custom_call_target="tpu_custom_call" | custom-call | tf_op jit(solution)/shard_map/exchange/pallas_call | solution.py:932
  68.1 5.2 %grads.1 = (f32[1024,1024]{1,0:T(8,128)}, f32[1024,1024]{1,0:T(8,128)}, f32[1024,1024]{1,0:T(8,128)}, bf16[1024,256]{1,0:T(8,128)(2,1)}) custom-call(bf16[128,1024]{1,0:T(8,128)(2,1)S(1)} %get-tuple-element.14.rows, bf16[128,1024]{1,0:T(8,128)(2,1)S(1)} %get-tuple-element.15.gate, bf16[128,1024]{1,0:T(8,128)(2,1)S(1)} %get-tuple-element.16.up, ...), custom_call_target="tpu_custom_call" | custom-call | tf_op jit(solution)/shard_map/grads/pallas_call | solution.py:963
Async XLA Ops:
  0.6 1.0 %copy-start = (bf16[256,512]{1,0:T(8,128)(2,1)S(1)}, bf16[256,512]{1,0:T(8,128)(2,1)}, u32[]{:S(2)}) copy-start(bf16[256,512]{1,0:T(8,128)(2,1)} %refs_4_.1) | copy-start | bytes 786436
  1.6 0.7 copy-start.1
  2.3 0.7 copy-start.2

commit v3 on v2

--- a/solution.py
+++ b/solution.py
@@ -20,7 +20,7 @@
     "attn", "out_weight", "residual", "projector", "student", "gain", "w_gate", "w_up",
     "w_down", "route", "o_rows", "o_gate", "o_up", "o_grad", "o_hidden", "o_teacher",
     "attn_v", "weight_v", "resid_v", "proj_v", "stud_v", "wg", "wu", "wd", "route_v", "gain_v",
-    "load_sem",
+    "load_sem", "out_sem",
     "q_send", "q_land", "q_sem", "t_send", "t_land", "r_acc", "r_land", "f_acc", "f_land", "t_sem", "r_sem", "f_sem",
     "c_send", "c_land", "p_acc", "p_land", "p_keep", "p_send", "p_zland", "c_sem", "p_sem", "z2_sem",
     "x_land", "sq_send", "sq_land", "count_land", "x_sem", "sq_sem", "count_sem", "z_send",
@@ -28,19 +28,6 @@
     "gh_land", "gh_share", "gh_sem", "part", "m_send", "m_land", "v_share", "v_land", "m_sem",
     "v_sem", "grad_v", "g_sem",
 )
-PROFILE = False
-open_scope = []
-
-
-def mark(name):
-    if not PROFILE:
-        return
-    while open_scope:
-        open_scope.pop().__exit__(None, None, None)
-    if name:
-        scope = jax.named_scope(name)
-        scope.__enter__()
-        open_scope.append(scope)
 
 
 def contract(left, right, left_dim, right_dim):
@@ -104,7 +91,7 @@
         return remote(
             self.share.at[way, chunk],
             self.land.at[way, chunk],
-            self.send_sem.at[way, chunk],
+            self.send_sem.at[way],
             self.recv_sem.at[way, chunk],
             batch=peer,
         )
@@ -147,8 +134,14 @@
     def drain(self):
         for late in (False, True):
             way, _, after, peer = self.flow(late)
-            for chunk in range(self.chunks):
-                wait_send_if(after, self.copy(way, chunk, peer))
+            every = remote(
+                self.share.at[way],
+                self.land.at[way],
+                self.send_sem.at[way],
+                self.recv_sem.at[way, 0],
+                batch=peer,
+            )
+            wait_send_if(after, every)
 
 
 class PlaneScatter:
@@ -185,7 +178,7 @@
         return remote(
             self.acc.at[self.place(block), half],
             self.land.at[slot, half],
-            self.send_sem.at[slot, half],
+            self.send_sem,
             self.recv_sem.at[slot, half],
             tensor=2 * xor(self.chip, flip, self.bits) + self.core,
         )
@@ -219,10 +212,10 @@
         return value
 
     def drain(self):
-        for half in range(2):
-            for stage in range(self.bits):
-                for block in self.stages[half][stage][1]:
-                    self.copy(half, stage, block).wait_send()
+        every = remote(
+            self.land, self.land, self.send_sem, self.recv_sem.at[0, 0], tensor=self.core
+        )
+        every.wait_send()
 
 
 def exchange_kernel(dims, *refs):
@@ -248,7 +241,6 @@
     portion = slots // chips
     others = range(1, chips)
 
-    mark("a_loads")
     loads = {}
 
     def load(name, src, dst):
@@ -305,7 +297,6 @@
             device_id_type=pl.DeviceIdType.MESH,
         )
 
-    mark("b_route")
     loads["route"].wait()
     route = r.route_v[...]
     row_id = lax.broadcasted_iota(jnp.int32, (slots, slots), 0)
@@ -319,16 +310,14 @@
     loads["student"].wait()
     r.x_land[0] = contract(pick, r.stud_v[...], 1, 0).astype(bf16)
 
-    mark("c_barrier")
     pl.semaphore_wait(barrier, chips - 1 + 1 + groups - 1)
 
-    mark("d_tprep")
     x_copies = [
         remote(
             r.x_land.at[0],
             r.x_land.at[step],
-            r.x_sem.at[0, step],
-            r.x_sem.at[1, step],
+            r.out_sem.at[0],
+            r.x_sem.at[step],
             tensor=2 * xor(chip, step, bits) + core,
         )
         for step in others
@@ -340,8 +329,8 @@
         return remote(
             r.count_land.at[b],
             r.count_land.at[b],
-            r.count_sem.at[0, step],
-            r.count_sem.at[1, b],
+            r.out_sem.at[1],
+            r.count_sem.at[b],
             batch=lax.rem(b + step, groups),
         )
 
@@ -352,12 +341,13 @@
     all_rows = slice(slots, slots + tokens)
     r.attn_v[0:slots] = contract(pick, r.attn_v[all_rows], 1, 0).astype(bf16)
 
-    def pair_copy(send, land, sem, relative):
+    def pair_copy(send, land, sems, relative):
+        out, sem = sems
         return remote(
             send.at[relative],
             land.at[relative],
-            sem.at[0, relative],
-            sem.at[1, relative],
+            r.out_sem.at[out],
+            sem.at[relative],
             tensor=partner,
         )
 
@@ -385,15 +375,14 @@
             for half in range(2):
                 acc[relative, half, :, span] = value[half * count : (half + 1) * count]
 
-    few = (slice(0, slots), r.q_send, r.q_land, r.q_sem)
-    many = (all_rows, r.t_send, r.t_land, r.t_sem)
+    few = (slice(0, slots), r.q_send, r.q_land, (2, r.q_sem))
+    many = (all_rows, r.t_send, r.t_land, (3, r.t_sem))
     routed_sum = PlaneScatter(
-        r.r_acc, r.r_land, r.r_sem.at[0], r.r_sem.at[1], chip, core, bits
+        r.r_acc, r.r_land, r.out_sem.at[5], r.r_sem, chip, core, bits
     )
     full_sum = PlaneScatter(
-        r.f_acc, r.f_land, r.f_sem.at[0], r.f_sem.at[1], chip, core, bits
-    )
-    mark("e_away")
+        r.f_acc, r.f_land, r.out_sem.at[6], r.f_sem, chip, core, bits
+    )
     for step in range(chips):
         loads[("w", step)].wait()
         away(*few, step)
@@ -402,7 +391,6 @@
         home(*few, r.r_acc, step)
     routed_sum.send(0)
 
-    mark("f_waitx")
     for copy in x_copies:
         copy.wait_recv()
     square = jnp.zeros((slots, 1), f32)
@@ -411,11 +399,10 @@
         square = square + jnp.sum(value * value, axis=1, keepdims=True)
     r.sq_send[...] = jnp.broadcast_to(square, r.sq_send.shape)
     sq_copy = remote(
-        r.sq_send, r.sq_land, r.sq_sem.at[0], r.sq_sem.at[1], tensor=partner
+        r.sq_send, r.sq_land, r.out_sem.at[15], r.sq_sem.at[0], tensor=partner
     )
     sq_copy.start()
     away(*many, 0)
-    mark("h_norm")
     sq_copy.wait_recv()
     square = r.sq_send[:, 0:1] + r.sq_land[:, 0:1]
     loads["gain"].wait()
@@ -425,8 +412,8 @@
         return remote(
             r.z_send.at[relative],
             r.z_land.at[b],
-            r.z_sem.at[0, relative],
-            r.z_sem.at[1, b],
+            r.out_sem.at[8],
+            r.z_sem.at[b],
             batch=peer,
         )
 
@@ -445,31 +432,26 @@
             r.z_send[relative] = value
             z_copy(relative, peer).start()
 
-    mark("i_home")
     for step in range(1, chips):
         away(*many, step)
     home(*many, r.f_acc, 0)
-    mark("j_rrecv")
     routed_sum.receive(0)
     routed_sum.send(1)
     for stage in range(2, bits):
         routed_sum.receive(stage - 1)
         routed_sum.send(stage)
     full_sum.send(0, 0, 1)
-    mark("j2_home")
     for step in range(1, chips):
         home(*many, r.f_acc, step)
 
-    mark("k_waitz")
     for group in range(groups):
         for land, sem in ((r.count_land, r.count_sem), (r.z_land, r.z_sem)):
             wait_recv_if(
                 group != b,
                 remote(
-                    land.at[group], land.at[group], sem.at[0, 0], sem.at[1, group], batch=b
+                    land.at[group], land.at[group], r.out_sem.at[0], sem.at[group], batch=b
                 ),
             )
-    mark("l_pack")
     pack_row = lax.broadcasted_iota(jnp.int32, (routed, slots), 0).astype(f32)
     pack_col = lax.broadcasted_iota(jnp.int32, (routed, slots), 1).astype(f32)
     mine_row = lax.broadcasted_iota(jnp.int32, (routed, portion), 0).astype(f32)
@@ -486,45 +468,46 @@
         offset = offset + amount
     r.rows_v[core] = packed.astype(bf16)
     row_copy = remote(
-        r.rows_v.at[core], r.rows_v.at[core], r.row_sem.at[0], r.row_sem.at[1], tensor=partner
+        r.rows_v.at[core], r.rows_v.at[core], r.out_sem.at[16], r.row_sem.at[0], tensor=partner
     )
     row_copy.start()
 
-    mark("m_proj1")
     loads["w_gate"].wait()
     loads["w_up"].wait()
+
+    out_gu = r.out_sem.at[pl.ds(10, 2)]
+    gate_up = Chain(r.gu, r.gu_land, r.gu_share, out_gu, r.gu_sem, b, groups)
 
     def project(side, first):
         start = pl.multiple_of(side * width, width)
         rows = r.rows_v[side]
-        for chunk in range(chunks):
-            span = slice(chunk * cols, (chunk + 1) * cols)
+        for first_chunk in range(0, chunks, 2):
+            span = slice(first_chunk * cols, (first_chunk + 2) * cols)
             for which, weight in enumerate((r.wg, r.wu)):
                 value = jnp.dot(
                     rows, weight[pl.ds(start, width), span], preferred_element_type=f32
                 )
-                for turn in range(2):
-                    item = turn * chunks + chunk
-                    piece = value[turn * tall : (turn + 1) * tall]
+                for turn, side_chunk in ((0, 0), (0, 1), (1, 0), (1, 1)):
+                    item = turn * chunks + first_chunk + side_chunk
+                    piece = value[
+                        turn * tall : (turn + 1) * tall,
+                        side_chunk * cols : (side_chunk + 1) * cols,
+                    ]
                     r.gu[item, which] = piece if first else r.gu[item, which] + piece
 
     project(core, True)
-    mark("o_rowwait")
     remote(
         r.rows_v.at[1 - core],
         r.rows_v.at[1 - core],
+        r.out_sem.at[16],
         r.row_sem.at[0],
-        r.row_sem.at[1],
         tensor=partner,
     ).wait_recv()
-    mark("p_proj2")
     project(1 - core, False)
-    gate_up = Chain(r.gu, r.gu_land, r.gu_share, r.gu_sem.at[0], r.gu_sem.at[1], b, groups)
     gate_up.origin(0, chunks)
     for side in range(2):
         r.o_rows[:, side * width : (side + 1) * width] = r.rows_v[side]
 
-    mark("r_rrecv1")
     routed_sum.receive(bits - 1)
     loads["residual"].wait()
     routed_resid = contract(pick, r.resid_v[...], 1, 1)
@@ -534,21 +517,19 @@
         r.p_keep[first : first + slots // 2] = value.astype(bf16)
 
     def target_copy(relative):
-        return pair_copy(r.c_send, r.c_land, r.c_sem, relative)
-
-    mark("s_target")
+        return pair_copy(r.c_send, r.c_land, (4, r.c_sem), relative)
+
     for step in range(groups):
         loads[("p", step)].wait()
         value = jnp.dot(r.p_keep[...], r.proj_v[step], preferred_element_type=f32)
         r.c_send[step] = value.astype(bf16)
         target_copy(step).start()
     target_sum = PlaneScatter(
-        r.p_acc, r.p_land, r.p_sem.at[0], r.p_sem.at[1], chip, core, bits, absolute=True
+        r.p_acc, r.p_land, r.out_sem.at[7], r.p_sem, chip, core, bits, absolute=True
     )
     side_blocks = groups // 2
 
     def target_home():
-        mark("u_target2")
         for step in range(groups):
             loads[("p", groups + step)].wait()
             value = jnp.dot(r.p_keep[...], r.proj_v[groups + step], preferred_element_type=f32)
@@ -561,7 +542,6 @@
         target_sum.send(0)
 
     def target_relay():
-        mark("v_trelay")
         for stage in range(1, bits):
             target_sum.receive(stage - 1)
             target_sum.send(stage)
@@ -570,13 +550,12 @@
         return remote(
             r.p_send.at[peer],
             r.p_zland.at[b],
-            r.z2_sem.at[0, peer],
-            r.z2_sem.at[1, b],
+            r.out_sem.at[9],
+            r.z2_sem.at[b],
             batch=peer,
         )
 
     def target_end():
-        mark("x_tz")
         target_sum.receive(bits - 1)
         for half in range(2):
             value = target_sum.final(half).astype(bf16)
@@ -596,7 +575,6 @@
         full_sum.send(0, 1)
 
     def down(turn):
-        mark(f"y_down{turn}")
         rows = slice(turn * tall, (turn + 1) * tall)
         if turn == 0:
             loads["w_down"].wait()
@@ -606,9 +584,11 @@
             gate, up = r.gu[item, 0], r.gu[item, 1]
             value = (gate * jax.nn.sigmoid(gate) * up).astype(bf16)
             r.o_hidden[rows, chunk * cols : (chunk + 1) * cols] = value
-        r.part[turn] = contract(r.o_hidden[rows], r.wd[...], 1, 1)
-
-        mark(f"z_tarrive{turn}")
+            if chunk % 2:
+                span = slice((chunk - 1) * cols, (chunk + 1) * cols)
+                value = contract(r.o_hidden[rows, span], r.wd[:, span], 1, 1)
+                r.part[turn] = value if chunk == 1 else r.part[turn] + value
+
         value = jnp.zeros((tall, width), f32)
         for group in range(groups):
             if turn == 0:
@@ -617,8 +597,8 @@
                     remote(
                         r.p_zland.at[group],
                         r.p_zland.at[group],
-                        r.z2_sem.at[0, 0],
-                        r.z2_sem.at[1, group],
+                        r.out_sem.at[9],
+                        r.z2_sem.at[group],
                         batch=b,
                     ),
                 )
@@ -635,8 +615,8 @@
         return remote(
             r.m_send.at[turn],
             r.m_land.at[turn],
-            r.m_sem.at[0, turn],
-            r.m_sem.at[1, turn],
+            r.out_sem.at[17 + turn],
+            r.m_sem.at[turn],
             tensor=partner,
         )
 
@@ -645,8 +625,8 @@
         return remote(
             r.v_share.at[turn, stage, half],
             r.v_land.at[turn, stage, half],
-            r.v_sem.at[0, turn, stage, half],
-            r.v_sem.at[1, turn, stage, half],
+            r.out_sem.at[14],
+            r.v_sem.at[turn, stage, half],
             tensor=2 * xor(chip, 1 << bit, bits) + core,
         )
 
@@ -654,18 +634,16 @@
         return remote(
             r.grad_v.at[turn, side],
             r.grad_v.at[turn, side],
-            r.g_sem.at[0, turn],
-            r.g_sem.at[1, turn],
+            r.out_sem.at[19 + turn],
+            r.g_sem.at[turn],
             tensor=partner,
         )
 
     def misfit_start(turn):
-        mark(f"za_misfit{turn}")
         r.m_send[turn] = r.part[turn, given].astype(bf16)
         misfit_copy(turn).start()
 
     def double_start(turn, stage):
-        mark(f"zb_dstart{turn}{stage}")
         if stage == 0:
             misfit_copy(turn).wait_recv()
             total = r.part[turn, kept] + r.m_land[turn].astype(f32)
@@ -687,31 +665,30 @@
         return values
 
     def grad_start(turn):
-        mark(f"zc_gstart{turn}")
         values = doubled(turn, bits - 1)
         for half in range(2):
             span = slice(half * half_cols, (half + 1) * half_cols)
             r.grad_v[turn, core, :, span] = (values[half] * loss_scale).astype(bf16)
         grad_copy(turn, core).start()
 
-    grad_hidden = Chain(r.gh, r.gh_land, r.gh_share, r.gh_sem.at[0], r.gh_sem.at[1], b, groups)
+    out_gh = r.out_sem.at[pl.ds(12, 2)]
+    grad_hidden = Chain(r.gh, r.gh_land, r.gh_share, out_gh, r.gh_sem, b, groups)
 
     def back(turn):
-        mark(f"zd_back{turn}")
         grad_copy(turn, 1 - core).wait_recv()
         for side in range(2):
             first = turn * tall + side * short
             r.o_grad[first : first + short] = r.grad_v[turn, side]
         rows = slice(turn * tall, (turn + 1) * tall)
-        for chunk in range(chunks):
-            span = slice(chunk * cols, (chunk + 1) * cols)
-            r.gh[turn * chunks + chunk] = jnp.dot(
-                r.o_grad[rows], r.wd[:, span], preferred_element_type=f32
-            )
+        for chunk in range(0, chunks, 2):
+            span = slice(chunk * cols, (chunk + 2) * cols)
+            value = jnp.dot(r.o_grad[rows], r.wd[:, span], preferred_element_type=f32)
+            for side in range(2):
+                item = turn * chunks + chunk + side
+                r.gh[item] = value[:, side * cols : (side + 1) * cols]
         grad_hidden.origin(turn * chunks, (turn + 1) * chunks)
 
     def last(turn):
-        mark(f"zf_elem{turn}")
         rows = slice(turn * tall, (turn + 1) * tall)
         for chunk in range(chunks):
             item = turn * chunks + chunk
@@ -726,7 +703,6 @@
 
     def steps(chain, *items):
         for late, item in items:
-            mark(f"chain{'gh' if chain is grad_hidden else 'gu'}{late}{item}")
             chain.step(item, bool(late))
 
     def order_of(first, final, skew):
@@ -744,9 +720,9 @@
 
     target_home()
     gate_up.origin(chunks, items)
-    steps(gate_up, *order[: late[0] - 3])
+    steps(gate_up, *order[: late[0] - 1])
     target_relay()
-    steps(gate_up, *order[late[0] - 3 : late[chunks - 3]])
+    steps(gate_up, *order[late[0] - 1 : late[chunks - 3]])
     target_end()
     begin = min(items - 2, chunks + 1)
     steps(gate_up, *order[late[chunks - 3] : late[begin]])
@@ -771,50 +747,45 @@
         double_start(1, stage)
     steps(grad_hidden, *order[2 : late[0] - 1])
     grad_start(1)
-    steps(grad_hidden, *order[late[0] - 1 : late[3]])
-    back(1)
-    mark("zg_full0")
     for stage in range(1, bits):
         full_sum.receive(stage - 1)
         full_sum.send(stage)
+    steps(grad_hidden, *order[late[0] - 1 : late[3]])
+    back(1)
     steps(grad_hidden, *order[late[3] :])
     last(0)
     steps(grad_hidden, *order_of(chunks, items, chunks))
     last(1)
 
-    mark("zg_full")
     full_sum.receive(bits - 1)
     for half in range(2):
         span = slice(half * (tokens // 2), (half + 1) * (tokens // 2))
         value = full_sum.final(half).T + r.resid_v[:, span].astype(f32)
         r.o_teacher[:, span] = value.astype(bf16)
 
-    mark("zh_drain")
-    for copy in x_copies:
-        copy.wait_send()
-    for step in range(1, groups):
-        count_copy(step).wait_send()
-    for relative in range(chips):
-        for send, land, sem in (few[1:], many[1:], (r.c_send, r.c_land, r.c_sem)):
-            pair_copy(send, land, sem, relative).wait_send()
-        peer = xor(chip, relative, bits)
-        wait_send_if(peer != b, z_copy(relative, peer))
-    for peer in range(groups):
-        wait_send_if(peer != b, target_z(peer))
+    some = pl.ds(1, chips - 1)
+    sent = (
+        (0, r.x_land.at[some]),
+        (1, r.count_land.at[some]),
+        (2, r.q_send),
+        (3, r.t_send),
+        (4, r.c_send),
+        (8, r.z_send.at[some]),
+        (9, r.p_send.at[some]),
+        (14, r.v_share),
+    )
+    for out, array in sent:
+        remote(array, array, r.out_sem.at[out], r.sq_sem.at[0], tensor=partner).wait_send()
     sq_copy.wait_send()
     row_copy.wait_send()
     for turn in range(2):
         misfit_copy(turn).wait_send()
         grad_copy(turn, core).wait_send()
-        for stage in range(bits):
-            for half in range(2):
-                double_copy(turn, stage, half).wait_send()
     routed_sum.drain()
     target_sum.drain()
     full_sum.drain()
     gate_up.drain()
     grad_hidden.drain()
-    mark(None)
 
 
 def grads_kernel(
@@ -876,18 +847,19 @@
         pltpu.VMEM(route_index.shape, route_index.dtype),
         pltpu.VMEM((1, model), f32),
         dma((8 + 2 * tensors,)),
+        dma((21,)),
         pltpu.VMEM((chips, slots, feats), bf16),
         pltpu.VMEM((chips, slots, feats), bf16),
-        dma((2, chips)),
+        dma((chips,)),
         pltpu.VMEM((chips, tokens, feats), bf16),
         pltpu.VMEM((chips, tokens, feats), bf16),
         pltpu.VMEM((chips, 2, slots // 2, feats), bf16),
         pltpu.VMEM((moved, 2, slots // 2, feats), bf16),
         pltpu.VMEM((chips, 2, tokens // 2, feats), bf16),
         pltpu.VMEM((moved, 2, tokens // 2, feats), bf16),
-        dma((2, chips)),
-        dma((2, moved, 2)),
-        dma((2, moved, 2)),
+        dma((chips,)),
+        dma((moved, 2)),
+        dma((moved, 2)),
         pltpu.VMEM((chips, slots, width), bf16),
         pltpu.VMEM((chips, slots, width), bf16),
         pltpu.VMEM((chips, 2, slots // chips, model // 4), bf16),
@@ -895,39 +867,39 @@
         pltpu.VMEM((slots, feats), bf16),
         pltpu.VMEM((groups, slots // chips, width), bf16),
         pltpu.VMEM((groups, slots // chips, width), bf16),
-        dma((2, chips)),
-        dma((2, moved, 2)),
-        dma((2, groups)),
+        dma((chips,)),
+        dma((moved, 2)),
+        dma((groups,)),
         pltpu.VMEM((chips, slots, width), bf16),
         pltpu.VMEM((slots, 128), f32),
         pltpu.VMEM((slots, 128), f32),
         pltpu.VMEM((groups, 8, 128), f32),
-        dma((2, chips)),
+        dma((chips,)),
         dma((2,)),
-        dma((2, groups)),
+        dma((groups,)),
         pltpu.VMEM((chips, slots, width), bf16),
         pltpu.VMEM((groups, slots, width), bf16),
-        dma((2, max(chips, groups))),
+        dma((groups,)),
         pltpu.VMEM((groups, routed, slots // chips), bf16),
         pltpu.VMEM((2, routed, width), bf16),
         dma((2,)),
         pltpu.VMEM((2 * chunks, 2, routed // 2, cols), f32),
         pltpu.VMEM((2, 2 * chunks, 2, routed // 2, cols), bf16),
         pltpu.VMEM((2, 2 * chunks, 2, routed // 2, cols), bf16),
-        dma((2, 2, 2 * chunks)),
+        dma((2, 2 * chunks)),
         pltpu.VMEM((2 * chunks, routed // 2, cols), f32),
         pltpu.VMEM((2, 2 * chunks, routed // 2, cols), bf16),
         pltpu.VMEM((2, 2 * chunks, routed // 2, cols), bf16),
-        dma((2, 2, 2 * chunks)),
+        dma((2, 2 * chunks)),
         pltpu.VMEM((2, routed // 2, block), f32),
         pltpu.VMEM((2, routed // 4, block), bf16),
         pltpu.VMEM((2, routed // 4, block), bf16),
         pltpu.VMEM((2, bits, 2, routed // 4, block // 2), bf16),
         pltpu.VMEM((2, bits, 2, routed // 4, block // 2), bf16),
-        dma((2, 2)),
-        dma((2, 2, bits, 2)),
+        dma((2,)),
+        dma((2, bits, 2)),
         pltpu.VMEM((2, 2, routed // 4, block), bf16),
-        dma((2, 2)),
+        dma((2,)),
     ]
     rows, gate, up, grad, hidden, teacher = pl.pallas_call(
         functools.partial(exchange_kernel, (groups, tensors, mean_routed)),

time: 73.6 us -> 72.1 us (0.980)
  Pallas kernels: 70.3 us -> 68.7 us
    pallas_call x1, Pallas kernels: 65.1 us -> 63.5 us  [on_device(): pl.pallas_call(functools.partial(exchange_kernel, (groups, tensors, mean_...]
where the time goes in v3:
time: 72.1 us; the launch traced here: 71.8 us
  Pallas kernels  68.7 us (95%)
  local copies, waits for them, and re-layouts  2.31 us (3%)
  between operations  0.81 us (1%)
    pallas_call x1, Pallas kernels, on_device(): pl.pallas_call(functools.partial(exchange_kernel, (groups, tensors, mean_...  63.5 us
    pallas_call x1, Pallas kernels, on_device(): pl.pallas_call(grads_kernel, name='grads', out_shape=(grads, grads, grads...  5.15 us
    unnamed x6, local copies, waits for them, and re-layouts  2.31 us

profile of v3, /device:TPU:0, one launch (start us, length us, event | category | flops | bytes accessed | tf_op | source)
XLA Modules:
  0.0 71.8 jit_solution(2563726030138261497)
XLA Ops:
  0.6 0.0 copy-start
  0.6 0.9 %copy-done = bf16[256,512]{1,0:T(8,128)(2,1)S(1)} copy-done((bf16[256,512]{1,0:T(8,128)(2,1)S(1)}, bf16[256,512]{1,0:T(8,128)(2,1)}, u32[]{:S(2)}) %copy-start) | copy-done | bytes 262168
  1.6 0.0 copy-start.1
  1.6 0.7 copy-done.1
  2.3 0.0 copy-start.2
  2.3 0.7 copy-done.2
  3.0 63.5 %exchange.1 = (bf16[128,1024]{1,0:T(8,128)(2,1)S(1)}, bf16[128,1024]{1,0:T(8,128)(2,1)S(1)}, bf16[128,1024]{1,0:T(8,128)(2,1)S(1)}, bf16[128,1024]{1,0:T(8,128)(...) custom-call(bf16[256,1024]{1,0:T(8,128)(2,1)} %refs_0_.1, bf16[1024,8192]{1,0:T(8,128)(2,1)} %refs_1_.1, ...), custom_call_target="tpu_custom_call" | custom-call | tf_op jit(solution)/shard_map/exchange/pallas_call | solution.py:904
  66.5 5.2 %grads.1 = (f32[1024,1024]{1,0:T(8,128)}, f32[1024,1024]{1,0:T(8,128)}, f32[1024,1024]{1,0:T(8,128)}, bf16[1024,256]{1,0:T(8,128)(2,1)}) custom-call(bf16[128,1024]{1,0:T(8,128)(2,1)S(1)} %get-tuple-element.14.rows, bf16[128,1024]{1,0:T(8,128)(2,1)S(1)} %get-tuple-element.15.gate, bf16[128,1024]{1,0:T(8,128)(2,1)S(1)} %get-tuple-element.16.up, ...), custom_call_target="tpu_custom_call" | custom-call | tf_op jit(solution)/shard_map/grads/pallas_call | solution.py:935
Async XLA Ops:
  0.6 1.0 %copy-start = (bf16[256,512]{1,0:T(8,128)(2,1)S(1)}, bf16[256,512]{1,0:T(8,128)(2,1)}, u32[]{:S(2)}) copy-start(bf16[256,512]{1,0:T(8,128)(2,1)} %refs_4_.1) | copy-start | bytes 786436
  1.6 0.7 copy-start.1
  2.3 0.7 copy-start.2

commit v4 on v3

--- a/solution.py
+++ b/solution.py
@@ -930,7 +930,7 @@
         w_down,
         route_index,
     )
-    parts = 4
+    parts = block // 128
     grads = jax.ShapeDtypeStruct((block, units), f32)
     grad_gate, grad_up, grad_down, teacher_hidden = pl.pallas_call(
         grads_kernel,

time: 72.1 us -> 72.1 us (level)
  no operation moved by 1% of the time
where the time goes in v4:
time: 72.1 us; the launch traced here: 71.8 us
  Pallas kernels  68.7 us (95%)
  local copies, waits for them, and re-layouts  2.31 us (3%)
  between operations  0.81 us (1%)
    pallas_call x1, Pallas kernels, on_device(): pl.pallas_call(functools.partial(exchange_kernel, (groups, tensors, mean_...  63.5 us
    pallas_call x1, Pallas kernels, on_device(): pl.pallas_call(grads_kernel, name='grads', out_shape=(grads, grads, grads...  5.17 us
    unnamed x6, local copies, waits for them, and re-layouts  2.31 us

profile of v4, /device:TPU:0, one launch (start us, length us, event | category | flops | bytes accessed | tf_op | source)
XLA Modules:
  0.0 71.8 jit_solution(989375640390889825)
XLA Ops:
  0.6 0.0 copy-start
  0.6 0.9 %copy-done = bf16[256,512]{1,0:T(8,128)(2,1)S(1)} copy-done((bf16[256,512]{1,0:T(8,128)(2,1)S(1)}, bf16[256,512]{1,0:T(8,128)(2,1)}, u32[]{:S(2)}) %copy-start) | copy-done | bytes 262168
  1.6 0.0 copy-start.1
  1.6 0.7 copy-done.1
  2.3 0.0 copy-start.2
  2.3 0.7 copy-done.2
  3.0 63.5 %exchange.1 = (bf16[128,1024]{1,0:T(8,128)(2,1)S(1)}, bf16[128,1024]{1,0:T(8,128)(2,1)S(1)}, bf16[128,1024]{1,0:T(8,128)(2,1)S(1)}, bf16[128,1024]{1,0:T(8,128)(...) custom-call(bf16[256,1024]{1,0:T(8,128)(2,1)} %refs_0_.1, bf16[1024,8192]{1,0:T(8,128)(2,1)} %refs_1_.1, ...), custom_call_target="tpu_custom_call" | custom-call | tf_op jit(solution)/shard_map/exchange/pallas_call | solution.py:904
  66.5 5.2 %grads.1 = (f32[1024,1024]{1,0:T(8,128)}, f32[1024,1024]{1,0:T(8,128)}, f32[1024,1024]{1,0:T(8,128)}, bf16[1024,256]{1,0:T(8,128)(2,1)}) custom-call(bf16[128,1024]{1,0:T(8,128)(2,1)S(1)} %get-tuple-element.14.rows, bf16[128,1024]{1,0:T(8,128)(2,1)S(1)} %get-tuple-element.15.gate, bf16[128,1024]{1,0:T(8,128)(2,1)S(1)} %get-tuple-element.16.up, ...), custom_call_target="tpu_custom_call" | custom-call | tf_op jit(solution)/shard_map/grads/pallas_call | solution.py:935
Async XLA Ops:
  0.6 1.0 %copy-start = (bf16[256,512]{1,0:T(8,128)(2,1)S(1)}, bf16[256,512]{1,0:T(8,128)(2,1)}, u32[]{:S(2)}) copy-start(bf16[256,512]{1,0:T(8,128)(2,1)} %refs_4_.1) | copy-start | bytes 786436
  1.6 0.7 copy-start.1
  2.3 0.7 copy-start.2
